TPU v7x, 32 devices: a whole 2x2x4 slice. The times are simulated.
32 devices in a mesh: grp: 2 (over y), lon: 4 (over z), lat: 2 (over x), lvl: 2 (over core).
Axes of the slice: x: 2, y: 2, z: 4, core: 2. Of those that a mesh axis runs over, the one named last changes fastest.
Arguments:
- tokens: bfloat16 [4, 24, 96, 512], P(('grp', 'lvl'), 'lat', 'lon'), parts along dimension 0, may hold values from -8 to 8
- fine_tags: int32 [4, 24, 96], P(('grp', 'lvl'), 'lat', 'lon'), parts along dimension 0, may hold values from 1 to 3
- coarse_tags: int32 [4, 12, 48], P(('grp', 'lvl'), 'lat', 'lon'), parts along dimension 0, may hold values from 1 to 3
- fine_gain: float32 [512], replicated, may hold values from 0.25 to 1.75
- fine_inward: bfloat16 [3, 512, 512], P(None, 'lon', 'lvl'), may hold values from -0.25 to 0.25
- fine_outward: bfloat16 [512, 512], P('lon', 'lvl'), may hold values from -0.25 to 0.25
- fine_table: float32 [16, 253], replicated, may hold values from -2 to 300
- merge_gain: float32 [2048], replicated, may hold values from 0.25 to 1.75
- merge_weight: bfloat16 [1024, 2048], P('lon', 'lvl'), may hold values from -0.125 to 0.125
- coarse_gain: float32 [1024], replicated, may hold values from 0.25 to 1.75
- coarse_inward: bfloat16 [3, 1024, 1024], P(None, 'lon', 'lvl'), may hold values from -0.1875 to 0.1875
- coarse_outward: bfloat16 [1024, 1024], P('lon', 'lvl'), may hold values from -0.1875 to 0.1875
- coarse_table: float32 [32, 253], replicated, may hold values from -2 to 300
Outputs:
- fine_out: bfloat16 [4, 24, 96, 512], P(('grp', 'lvl'), 'lat', 'lon'), parts along dimension 0
- coarse_out: bfloat16 [4, 12, 48, 1024], P(('grp', 'lvl'), 'lat', 'lon'), parts along dimension 0
There are 2 independent parts, one for each index of `grp`. A program takes and returns all parts, laid end to end along the dimension named above; an argument that names none is the same for every part. Nothing has to cross between parts.
All inputs are finite; a program needn't handle non-finite values.
Results may differ from a plain program's by a relative error of at most 0.017.
Values may be sent and summed in bfloat16 or wider, within the bound.
A program may use at most 64 MiB of HBM per device.

v0:
```python
import jax
import jax.numpy as jnp
from jax import lax
from jax.sharding import PartitionSpec as P

WIN_LAT = 6
WIN_LON = 12


EPSILON = 1e-05


def padded(block, sides, width, periodic):
    for axis, dim in sides:
        count = lax.axis_size(axis)
        forward = [(i, i + 1) for i in range(count - 1)]
        if periodic:
            forward.append((count - 1, 0))
        backward = [(target, source) for source, target in forward]
        low = lax.ppermute(
            lax.slice_in_dim(block, block.shape[dim] - width, None, axis=dim), axis, forward
        )
        high = lax.ppermute(lax.slice_in_dim(block, 0, width, axis=dim), axis, backward)
        block = jnp.concatenate([low, block, high], axis=dim)
    return block


def layer_norm(values, scales):
    widened = values.astype(jnp.float32)
    center = widened - jnp.mean(widened, axis=-1, keepdims=True)
    spread = jnp.mean(center * center, axis=-1, keepdims=True)
    return center * lax.rsqrt(spread + EPSILON) * scales


def bias_blocks(bias_table, win_lat, win_lon):
    head_count = bias_table.shape[0]
    span_lat = 2 * win_lat - 1
    span_lon = 2 * win_lon - 1
    table_grid = bias_table.reshape(head_count, span_lat, span_lon)
    lat_pos = jnp.arange(win_lat)
    lon_pos = jnp.arange(win_lon)
    lat_onehot = (
        lat_pos[:, None, None] - lat_pos[None, :, None] + win_lat - 1
        == jnp.arange(span_lat)[None, None, :]
    ).astype(jnp.float32)
    lon_onehot = (
        lon_pos[:, None, None] - lon_pos[None, :, None] + win_lon - 1
        == jnp.arange(span_lon)[None, None, :]
    ).astype(jnp.float32)
    along_lon = jnp.einsum("hab,ijb->haij", table_grid, lon_onehot, precision=lax.Precision.HIGHEST)
    blocks = jnp.einsum("kla,haij->hkilj", lat_onehot, along_lon, precision=lax.Precision.HIGHEST)
    return blocks.reshape(head_count, win_lat * win_lon, win_lat * win_lon)


def split_windows(array_in, win_lat, win_lon):
    levels, lat_len, lon_len = array_in.shape[:3]
    trailing = array_in.shape[3:]
    blocked = array_in.reshape(
        (levels, lat_len // win_lat, win_lat, lon_len // win_lon, win_lon) + trailing
    )
    blocked = jnp.moveaxis(blocked, 3, 2)
    return blocked.reshape(
        (levels, lat_len // win_lat, lon_len // win_lon, win_lat * win_lon) + trailing
    )


def join_windows(array_in, win_lat, win_lon):
    levels, lat_bands, lon_bands = array_in.shape[:3]
    trailing = array_in.shape[4:]
    blocked = array_in.reshape((levels, lat_bands, lon_bands, win_lat, win_lon) + trailing)
    blocked = jnp.moveaxis(blocked, 3, 2)
    return blocked.reshape((levels, lat_bands * win_lat, lon_bands * win_lon) + trailing)


def attend(query_grid, key_grid, value_grid, tag_grid, bias_table, win_lat, win_lon):
    head_count = bias_table.shape[0]
    features = query_grid.shape[-1]
    head_size = features // head_count

    def heads_of(array_in):
        blocks = split_windows(array_in, win_lat, win_lon)
        return blocks.reshape(blocks.shape[:4] + (head_count, head_size))

    query_heads = heads_of(query_grid)
    key_heads = heads_of(key_grid)
    value_heads = heads_of(value_grid)
    scores = jnp.einsum(
        "zabphd,zabqhd->zabhpq", query_heads, key_heads, preferred_element_type=jnp.float32
    )
    scores = scores * head_size ** (-0.5) + bias_blocks(bias_table, win_lat, win_lon)
    tag_blocks = split_windows(tag_grid, win_lat, win_lon)
    allowed = tag_blocks[..., None, :, None] == tag_blocks[..., None, None, :]
    scores = jnp.where(allowed, scores, -jnp.inf)
    highest = jnp.max(scores, axis=-1, keepdims=True)
    weights = jnp.exp(scores - highest)
    shares = (weights / jnp.sum(weights, axis=-1, keepdims=True)).astype(jnp.bfloat16)
    blended = jnp.einsum(
        "zabhpq,zabqhd->zabphd", shares, value_heads, preferred_element_type=jnp.float32
    )
    blended = blended.astype(jnp.bfloat16).reshape(blended.shape[:4] + (features,))
    return join_windows(blended, win_lat, win_lon)


def project_rows(normed, inward, coarse):

    def accumulate(segment):
        return jnp.einsum("tc,kcg->tkg", normed, segment, preferred_element_type=jnp.float32)

    if coarse:
        summed = accumulate(lax.all_gather(inward, "lon", axis=1, tiled=True))
    else:
        summed = accumulate(lax.all_gather(inward, "lon", axis=1, tiled=True))
    return summed.astype(jnp.bfloat16)


def output_columns(blended, outward, coarse):

    def output_project(segment):
        return lax.dot_general(
            blended, segment, (((1,), (1,)), ((), ())), preferred_element_type=jnp.float32
        )

    if coarse:
        return output_project(lax.all_gather(outward, "lon", axis=0, tiled=True))
    return output_project(lax.all_gather(outward, "lon", axis=0, tiled=True))


def merge_columns(normed, merge_rows):
    return lax.dot_general(
        normed,
        lax.all_gather(merge_rows, "lon", axis=0, tiled=True),
        (((1,), (1,)), ((), ())),
        preferred_element_type=jnp.float32,
    )


def widen_tags(tag_grid, coarse):
    if coarse:
        beside_all = padded(tag_grid, (("lon", 2),), WIN_LON // 2, True)
        return padded(beside_all, (("lat", 1),), WIN_LAT // 2, False)
    beside_all = padded(tag_grid, (("lon", 2),), WIN_LON // 2, True)
    return padded(beside_all, (("lat", 1),), WIN_LAT // 2, False)


def widen_normed(normed, coarse):
    if coarse:
        beside_all = padded(normed, (("lon", 2),), WIN_LON // 2, True)
        return padded(beside_all, (("lat", 1),), WIN_LAT // 2, False)
    beside_all = padded(normed, (("lon", 2),), WIN_LON // 2, True)
    return padded(beside_all, (("lat", 1),), WIN_LAT // 2, False)


def window_attend(query_wide, key_wide, value_wide, wide_tags, bias_table, lat_len, lon_len):
    lat_half = WIN_LAT // 2
    lon_half = WIN_LON // 2
    blended = attend(query_wide, key_wide, value_wide, wide_tags, bias_table, WIN_LAT, WIN_LON)
    own = blended[:, :, lon_half : lon_half + lon_len]
    return own[:, lat_half : lat_half + lat_len]


def shifted_attention(normed, tag_grid, inward, outward, bias_table, coarse):
    levels, lat_len, lon_len, features = normed.shape
    wide_tags = widen_tags(tag_grid, coarse)
    wide_normed = widen_normed(normed, coarse)
    wide_shape = wide_normed.shape[:3]
    triple = project_rows(wide_normed.reshape(-1, features), inward, coarse)
    inner_width = triple.shape[2]
    query_wide = triple[:, 0].reshape(wide_shape + (inner_width,))
    key_wide = triple[:, 1].reshape(wide_shape + (inner_width,))
    value_wide = triple[:, 2].reshape(wide_shape + (inner_width,))
    blended = window_attend(
        query_wide, key_wide, value_wide, wide_tags, bias_table, lat_len, lon_len
    )
    return output_columns(blended.reshape(-1, inner_width), outward, coarse)


def group_patches(stream):
    levels, lat_len, lon_len, features = stream.shape
    blocked = stream.reshape(levels, lat_len // 2, 2, lon_len // 2, 2, features)
    blocked = jnp.moveaxis(blocked, 3, 2)
    return blocked.reshape(levels, lat_len // 2, lon_len // 2, 4 * features)


def residual_add(stream, update):
    return (stream.astype(jnp.float32) + update).astype(jnp.bfloat16)


def table_rows(bias_table):
    head_count = bias_table.shape[0] // lax.axis_size("lvl")
    return lax.dynamic_slice_in_dim(bias_table, lax.axis_index("lvl") * head_count, head_count, 0)


def shards(
    tokens,
    fine_tags,
    coarse_tags,
    fine_gain,
    fine_inward,
    fine_outward,
    fine_table,
    merge_gain,
    merge_weight,
    coarse_gain,
    coarse_inward,
    coarse_outward,
    coarse_table,
):
    normed = layer_norm(tokens, fine_gain).astype(jnp.bfloat16)
    normed_all, tags_all = (
        lax.all_gather(normed, "lvl", axis=0, tiled=True),
        lax.all_gather(fine_tags.astype(jnp.bfloat16), "lvl", axis=0, tiled=True),
    )
    partial_value = shifted_attention(
        normed_all, tags_all, fine_inward, fine_outward, table_rows(fine_table), False
    )
    update = lax.psum_scatter(
        partial_value.reshape(normed_all.shape[:3] + (-1,)).astype(jnp.bfloat16),
        "lvl",
        scatter_dimension=0,
        tiled=True,
    ).astype(jnp.float32)
    fine_result = residual_add(tokens, update)
    merged_normed = layer_norm(group_patches(fine_result), merge_gain).astype(jnp.bfloat16)
    halves = lax.all_to_all(merged_normed, "lvl", split_axis=3, concat_axis=0, tiled=True)
    partial_merge = merge_columns(halves.reshape(-1, halves.shape[-1]), merge_weight)
    coarse_in = lax.psum_scatter(
        partial_merge.reshape(halves.shape[:3] + (-1,)).astype(jnp.bfloat16),
        "lvl",
        scatter_dimension=0,
        tiled=True,
    )
    coarse_normed = layer_norm(coarse_in, coarse_gain).astype(jnp.bfloat16)
    coarse_all, coarse_tags_all = (
        lax.all_gather(coarse_normed, "lvl", axis=0, tiled=True),
        lax.all_gather(coarse_tags.astype(jnp.bfloat16), "lvl", axis=0, tiled=True),
    )
    partial_coarse = shifted_attention(
        coarse_all, coarse_tags_all, coarse_inward, coarse_outward, table_rows(coarse_table), True
    )
    coarse_update = lax.psum_scatter(
        partial_coarse.reshape(coarse_all.shape[:3] + (-1,)).astype(jnp.bfloat16),
        "lvl",
        scatter_dimension=0,
        tiled=True,
    ).astype(jnp.float32)
    return (fine_result, residual_add(coarse_in, coarse_update))


def solution(mesh):
    placed = (
        P(("grp", "lvl"), "lat", "lon", None),
        P(("grp", "lvl"), "lat", "lon"),
        P(("grp", "lvl"), "lat", "lon"),
        P(),
        P(None, "lon", "lvl"),
        P("lon", "lvl"),
        P(),
        P(),
        P("lon", "lvl"),
        P(),
        P(None, "lon", "lvl"),
        P("lon", "lvl"),
        P(),
    )
    return jax.shard_map(
        shards,
        mesh=mesh,
        in_specs=placed,
        out_specs=(P(("grp", "lvl"), "lat", "lon", None), P(("grp", "lvl"), "lat", "lon", None)),
        check_vma=False,
    )
```

profile of v0, /device:TPU:0, one launch (start us, length us, event | category | flops | bytes accessed | tf_op | source)
XLA Modules:
  0.0 296.8 jit_solution(6319207223619989767)
XLA Ops:
  21.5 3.8 %collective-permute-start.5 = (bf16[2,12,6]{2,1,0:T(8,128)(2,1)S(1)}, bf16[2,12,6]{2,1,0:T(8,128)(2,1)S(1)}, u32[]{:S(2)}, u32[]{:S(2)}) collective-permute-start(bf16[2,12,6]{2,1,0:T(8,128)(2,1)S(1)} %get-tuple-element.19), channel_id=1, source_target_pairs={{4,0},{8,4},{12,8},{0,12},{5,1},{9,5},{13,9},{1,13},{6,2},{10,6},{... | collective-permute-start | bytes 872 | tf_op jit(solution)/shard_map/ppermute | solution.py:23
  27.2 18.6 %all_gather.28 = bf16[3,512,256]{2,1,0:T(8,128)(2,1)} all-gather(bf16[3,128,256]{2,1,0:T(8,128)(2,1)} %param.17), channel_id=1, replica_groups=mesh['grp'=2,'lon'=4,'lat'=2,'lvl'=2] {'lon'}, dimensions={1}, use_global_device_ids=true | all-gather | bytes 983040 | tf_op jit(solution)/shard_map/all_gather | solution.py:112
  45.8 3.6 %collective-permute-start.6 = (bf16[2,3,36]{2,1,0:T(4,128)(2,1)S(1)}, bf16[2,3,36]{2,1,0:T(4,128)(2,1)S(1)}, u32[]{:S(2)}, u32[]{:S(2)}) collective-permute-start(bf16[2,3,36]{2,1,0:T(4,128)(2,1)S(1)} %get-tuple-element.16), channel_id=1, source_target_pairs={{0,2},{1,3},{4,6},{5,7},{8,10},{9,11},{12,14},{13,15},{16,18},{17,... | collective-permute-start | bytes 1304 | tf_op jit(solution)/shard_map/ppermute | solution.py:20
  50.8 14.6 %all_gather.30 = bf16[512,256]{1,0:T(8,128)(2,1)} all-gather(bf16[128,256]{1,0:T(8,128)(2,1)S(1)} %copy-done.8), channel_id=1, replica_groups=mesh['grp'=2,'lon'=4,'lat'=2,'lvl'=2] {'lon'}, dimensions={0}, use_global_device_ids=true | all-gather | bytes 327680 | tf_op jit(solution)/shard_map/all_gather | solution.py:125
  65.3 3.7 %copy.175 = f32[8,6,12,6,12]{2,1,4,3,0:T(8,128)} copy(f32[8,6,12,6,12]{4,3,1,2,0:T(8,128)S(1)} %convolution_bitcast_fusion.1) | data formatting | bytes 331776 | tf_op jit(solution)/shard_map/add | solution.py:90
  72.3 4.5 %collective-permute-start.2 = (bf16[2,3,36,512]{3,2,1,0:T(8,128)(2,1)S(1)}, bf16[2,3,36,512]{3,2,1,0:T(8,128)(2,1)S(1)}, u32[]{:S(2)}, u32[]{:S(2)}) collective-permute-start(bf16[2,3,36,512]{3,2,1,0:T(8,128)(2,1)S(1)} %get-tuple-element.8), channel_id=1, source_target_pairs={{0,2},{1,3},{4,6},{5,7},{8,10},{9,11},{12,14},{13,15},{16,18},{17,... | collective-permute-start | bytes 663560 | tf_op jit(solution)/shard_map/ppermute | solution.py:20
  80.5 4.4 %collective-permute-done.3 = bf16[2,3,36,512]{3,2,1,0:T(8,128)(2,1)S(1)} collective-permute-done((bf16[2,3,36,512]{3,2,1,0:T(8,128)(2,1)S(1)}, bf16[2,3,36,512]{3,2,1,0:T(8,128)(2,1)S(1)}, u32[]{:S(2)}, u32[]{:S(2)}) %collective-permute-start.3) | collective-permute-done | bytes 221216 | tf_op jit(solution)/shard_map/ppermute | solution.py:23
  112.6 3.4 %copy.142 = bf16[2,3,3,72,8,32]{5,4,0,3,2,1:T(8,128)(2,1)S(1)} copy(bf16[2,3,3,72,8,32]{3,5,4,2,1,0:T(8,128)(2,1)} %fusion.30) | data formatting | bytes 1327104 | tf_op jit(solution)/shard_map/convert_element_type | solution.py:100
  121.1 6.3 %reduce-scatter.4.cloned.1.call-done = bf16[1,12,24,512]{3,2,1,0:T(8,128)(2,1)} async-done(((bf16[2,12,24,512]{3,2,1,0:T(8,128)(2,1)}), bf16[1,12,24,512]{3,2,1,0:T(8,128)(2,1)}) %reduce-scatter.4.cloned.1.call-update) | async-done | bytes 294928 | tf_op jit(solution)/shard_map/reduce_scatter | solution.py:216
  131.7 4.6 %copy.146 = bf16[1,6,12,2048]{2,1,0,3:T(8,128)(2,1)} copy(bf16[1,6,12,2048]{3,0,2,1:T(2,128)(2,1)S(1)} %multiply_convert_fusion) | data formatting | bytes 589824 | tf_op jit(solution)/shard_map/convert_element_type | solution.py:223
  136.3 5.5 %reshape.241 = bf16[2,2,36864]{2,1,0:T(2,128)(2,1)S(1)} reshape(bf16[2048,1,6,12]{3,2,1,0:T(8,128)(2,1)} %bitcast.127) | data formatting | bytes 589824
  141.8 4.0 %all_to_all.15 = bf16[2,2,36864]{2,1,0:T(2,128)(2,1)S(1)} all-to-all(bf16[2,2,36864]{2,1,0:T(2,128)(2,1)S(1)} %reshape.241), channel_id=1, replica_groups=mesh['grp'=2,'lon'=4,'lat'=2,'lvl'=2] {'lvl'}, dimensions={0} | all-to-all | bytes 589824 | tf_op jit(solution)/shard_map/all_to_all | solution.py:224
  145.8 5.5 %reshape.242 = bf16[2048,1,6,12]{3,2,1,0:T(8,128)(2,1)} reshape(bf16[2,2,36864]{2,1,0:T(2,128)(2,1)S(1)} %all_to_all.15) | data formatting | bytes 589824
  151.3 4.4 %copy.148 = bf16[1,6,12,2,1024]{4,2,1,3,0:T(8,128)(2,1)S(1)} copy(bf16[1,6,12,2,1024]{2,1,4,3,0:T(8,128)(2,1)} %bitcast.128) | data formatting | bytes 589824 | tf_op jit(solution)/shard_map/all_to_all | solution.py:224
  155.7 11.2 %all-gather.4.cloned.1.call-done = bf16[1024,1024]{1,0:T(8,128)(2,1)} async-done(((bf16[256,1024]{1,0:T(8,128)(2,1)}), bf16[1024,1024]{1,0:T(8,128)(2,1)}) %all-gather.4.cloned.1.call-update) | async-done | bytes 2097168 | tf_op jit(solution)/shard_map/all_gather | solution.py:131
  173.0 3.6 %collective-permute-start.13 = (bf16[2,6,6]{2,1,0:T(8,128)(2,1)S(1)}, bf16[2,6,6]{2,1,0:T(8,128)(2,1)S(1)}, u32[]{:S(2)}, u32[]{:S(2)}) collective-permute-start(bf16[2,6,6]{2,1,0:T(8,128)(2,1)S(1)} %get-tuple-element.23), channel_id=1, source_target_pairs={{4,0},{8,4},{12,8},{0,12},{5,1},{9,5},{13,9},{1,13},{6,2},{10,6},{... | collective-permute-start | bytes 440 | tf_op jit(solution)/shard_map/ppermute | solution.py:23
  179.2 7.0 %convolution_bitcast_fusion = f32[16,6,12,6,12]{0,3,1,4,2:T(8,128)} fusion(f32[16,11,12,12,1]{1,0,4,3,2:T(8,128)S(1)} %copy.172, s32[6,6]{1,0:T(8,128)S(1)} %subtract_add_fusion.1), kind=kOutput, calls=%fused_computation.31 | convolution fusion | flops 10949004 | bytes 433296 | tf_op jit(solution)/shard_map/kla,haij->hkilj/dot_general | solution.py:51
  186.2 7.1 %copy.180 = f32[16,6,12,6,12]{2,1,4,3,0:T(8,128)} copy(f32[16,6,12,6,12]{0,3,1,4,2:T(8,128)} %convolution_bitcast_fusion) | data formatting | bytes 663552 | tf_op jit(solution)/shard_map/add | solution.py:90
  193.3 4.1 %reshape.239 = f32[16,72,72]{1,2,0:T(8,128)} reshape(f32[16,6,12,6,12]{2,1,4,3,0:T(8,128)} %copy.180) | data formatting | bytes 663552 | tf_op jit(solution)/shard_map/add | solution.py:90
  203.0 3.8 %collective-permute-start.9 = (bf16[2,6,6,1024]{3,2,1,0:T(8,128)(2,1)S(1)}, bf16[2,6,6,1024]{3,2,1,0:T(8,128)(2,1)S(1)}, u32[]{:S(2)}, u32[]{:S(2)}) collective-permute-start(bf16[2,6,6,1024]{3,2,1,0:T(8,128)(2,1)S(1)} %get-tuple-element.15), channel_id=1, source_target_pairs={{4,0},{8,4},{12,8},{0,12},{5,1},{9,5},{13,9},{1,13},{6,2},{10,6},{... | collective-permute-start | bytes 442376 | tf_op jit(solution)/shard_map/ppermute | solution.py:23
  211.5 5.3 %collective-permute-done.8 = bf16[2,6,6,1024]{3,2,1,0:T(8,128)(2,1)S(1)} collective-permute-done((bf16[2,6,6,1024]{3,2,1,0:T(8,128)(2,1)S(1)}, bf16[2,6,6,1024]{3,2,1,0:T(8,128)(2,1)S(1)}, u32[]{:S(2)}, u32[]{:S(2)}) %collective-permute-start.8) | collective-permute-done | bytes 147488 | tf_op jit(solution)/shard_map/ppermute | solution.py:20
  216.8 6.1 %collective-permute-done.9 = bf16[2,6,6,1024]{3,2,1,0:T(8,128)(2,1)S(1)} collective-permute-done((bf16[2,6,6,1024]{3,2,1,0:T(8,128)(2,1)S(1)}, bf16[2,6,6,1024]{3,2,1,0:T(8,128)(2,1)S(1)}, u32[]{:S(2)}, u32[]{:S(2)}) %collective-permute-start.9) | collective-permute-done | bytes 147488 | tf_op jit(solution)/shard_map/ppermute | solution.py:23
  223.2 3.4 %collective-permute-start.10 = (bf16[2,3,24,1024]{3,2,1,0:T(8,128)(2,1)S(1)}, bf16[2,3,24,1024]{3,2,1,0:T(8,128)(2,1)S(1)}, u32[]{:S(2)}, u32[]{:S(2)}) collective-permute-start(bf16[2,3,24,1024]{3,2,1,0:T(8,128)(2,1)S(1)} %get-tuple-element.10), channel_id=1, source_target_pairs={{0,2},{1,3},{4,6},{5,7},{8,10},{9,11},{12,14},{13,15},{16,18},{17,... | collective-permute-start | bytes 884744 | tf_op jit(solution)/shard_map/ppermute | solution.py:20
  228.3 3.8 %collective-permute-done.10 = bf16[2,3,24,1024]{3,2,1,0:T(8,128)(2,1)S(1)} collective-permute-done((bf16[2,3,24,1024]{3,2,1,0:T(8,128)(2,1)S(1)}, bf16[2,3,24,1024]{3,2,1,0:T(8,128)(2,1)S(1)}, u32[]{:S(2)}, u32[]{:S(2)}) %collective-permute-start.10) | collective-permute-done | bytes 294944 | tf_op jit(solution)/shard_map/ppermute | solution.py:20
  232.1 4.1 %collective-permute-done.11 = bf16[2,3,24,1024]{3,2,1,0:T(8,128)(2,1)S(1)} collective-permute-done((bf16[2,3,24,1024]{3,2,1,0:T(8,128)(2,1)S(1)}, bf16[2,3,24,1024]{3,2,1,0:T(8,128)(2,1)S(1)}, u32[]{:S(2)}, u32[]{:S(2)}) %collective-permute-start.11) | collective-permute-done | bytes 294944 | tf_op jit(solution)/shard_map/ppermute | solution.py:23
  236.5 6.1 %all-gather.6.cloned.1.call-done = bf16[3,1024,512]{2,1,0:T(8,128)(2,1)} async-done(((bf16[3,256,512]{2,1,0:T(8,128)(2,1)}), bf16[3,1024,512]{2,1,0:T(8,128)(2,1)}) %all-gather.6.cloned.1.call-update) | async-done | bytes 3145744 | tf_op jit(solution)/shard_map/all_gather | solution.py:110
  242.6 3.9 %convolution_convert_fusion.1 = bf16[576,3,512]{2,0,1:T(8,128)(2,1)S(1)} fusion(bf16[576,1024,1]{1,0,2:T(8,128)(2,1)S(1)} %bitcast.139, bf16[3,1024,512]{2,1,0:T(8,128)(2,1)} %all-gather.6.cloned.1.call-done), kind=kOutput, calls=%fused_computation.32 | convolution fusion | flops 1812824064 | bytes 6094848 | tf_op jit(solution)/shard_map/tc,kcg->tkg/dot_general | solution.py:107
  252.7 4.3 %reshape_reshape.30 = bf16[2,2,2,72,16,32]{5,4,2,3,1,0:T(8,128)(2,1)} reshape(bf16[2,2,2,6,12,512]{5,2,4,3,1,0:T(2,128)(2,1)} %copy.154) | data formatting | bytes 1179648 | tf_op jit(solution)/shard_map/reshape;reshape | solution.py:82
  257.0 5.8 %fusion.15 = f32[2,2,2,16,72,72]{4,5,3,2,1,0:T(8,128)} fusion(bf16[2,2,2,72,16,32]{5,4,2,3,1,0:T(8,128)(2,1)} %reshape_reshape.30, bf16[2,2,2,72,16,32]{5,4,2,3,1,0:T(8,128)(2,1)S(1)} %reshape_reshape.29), kind=kOutput, calls=%fused_computation.22 | convolution fusion | flops 42467328 | bytes 3833856 | tf_op jit(solution)/shard_map/zabphd,zabqhd->zabhpq/dot_general | solution.py:87
  264.7 6.1 %fusion.82 = (f32[2,2,2,16,72]{4,3,2,1,0:T(8,128)S(1)}, f32[2,2,2,16,72,72]{4,5,3,2,1,0:T(8,128)S(1)}) fusion(f32[2,2,2,16,72,72]{4,5,3,2,1,0:T(8,128)} %fusion.15, f32[16,72,72]{1,2,0:T(8,128)} %reshape.239, pred[2,2,2,72,72]{3,4,2,1,0:T(8,128)(4,1)S(1)} %broadcast_compare_fusion.1), kind=kOutput, calls=%fused_computation.119 | output fusion | flops 5308487 | bytes 5718528 | tf_op jit(solution)/shard_map/sub | solution.py:95
  272.0 3.6 %copy.162 = bf16[2,2,2,72,16,32]{5,4,2,3,1,0:T(8,128)(2,1)S(1)} copy(bf16[2,2,2,72,16,32]{3,5,4,2,1,0:T(8,128)(2,1)S(1)} %fusion.33) | data formatting | bytes 1179648 | tf_op jit(solution)/shard_map/convert_element_type | solution.py:100
  280.7 6.6 %reduce-scatter.8.cloned.1.call-done = bf16[1,6,12,1024]{3,2,1,0:T(8,128)(2,1)} async-done(((bf16[2,6,12,1024]{3,2,1,0:T(8,128)(2,1)}), bf16[1,6,12,1024]{3,2,1,0:T(8,128)(2,1)}) %reduce-scatter.8.cloned.1.call-update) | async-done | bytes 147472 | tf_op jit(solution)/shard_map/reduce_scatter | solution.py:240
  (158 shorter events, 97.5 us)
Async XLA Ops:
  8.0 168.8 %copy-start = (f32[32,253]{1,0:T(8,128)S(1)}, f32[32,253]{1,0:T(8,128)}, u32[]{:S(2)}) copy-start(f32[32,253]{1,0:T(8,128)} %param.25) | copy-start | bytes 97156
  8.0 11.6 %copy-start.10 = (s32[1,12,24]{2,0,1:T(1,128)S(1)}, s32[1,12,24]{2,0,1:T(1,128)}, u32[]{:S(2)}) copy-start(s32[1,12,24]{2,0,1:T(1,128)} %param.14) | copy-start | bytes 3460
  8.0 17.3 %copy-start.12 = (f32[16,253]{1,0:T(8,128)S(1)}, f32[16,253]{1,0:T(8,128)}, u32[]{:S(2)}) copy-start(f32[16,253]{1,0:T(8,128)} %param.19) | copy-start | bytes 48580
  8.0 119.4 %reduce-scatter.4.cloned.1.call-start = ((), (), s32[]{:S(2)}) async-start(), calls=%async_computation.4 | async-start | bytes 884736 | tf_op jit(solution)/shard_map/reduce_scatter | solution.py:216
  14.7 36.1 %copy-start.8 = (bf16[128,256]{1,0:T(8,128)(2,1)S(1)}, bf16[128,256]{1,0:T(8,128)(2,1)}, u32[]{:S(2)}) copy-start(bf16[128,256]{1,0:T(8,128)(2,1)} %param.18) | copy-start | bytes 196612
  14.7 57.4 %collective-permute-start = (bf16[2,12,6,512]{3,2,1,0:T(8,128)(2,1)}, bf16[2,12,6,512]{3,2,1,0:T(8,128)(2,1)S(1)}, u32[]{:S(2)}, u32[]{:S(2)}) collective-permute-start(bf16[2,12,6,512]{3,2,1,0:T(8,128)(2,1)} %get-tuple-element.12), channel_id=1, source_target_pairs={{0,4},{4,8},{8,12},{12,0},{1,5},{5,9},{9,13},{13,1},{2,6},{6,10},{... | collective-permute-start | bytes 442376 | tf_op jit(solution)/shard_map/ppermute | solution.py:20
  17.6 54.5 %collective-permute-start.1 = (bf16[2,12,6,512]{3,2,1,0:T(8,128)(2,1)}, bf16[2,12,6,512]{3,2,1,0:T(8,128)(2,1)S(1)}, u32[]{:S(2)}, u32[]{:S(2)}) collective-permute-start(bf16[2,12,6,512]{3,2,1,0:T(8,128)(2,1)} %get-tuple-element.13), channel_id=1, source_target_pairs={{4,0},{8,4},{12,8},{0,12},{5,1},{9,5},{13,9},{1,13},{6,2},{10,6},{... | collective-permute-start | bytes 442376 | tf_op jit(solution)/shard_map/ppermute | solution.py:23
  21.5 24.2 %collective-permute-start.4 = (bf16[2,12,6]{2,1,0:T(8,128)(2,1)S(1)}, bf16[2,12,6]{2,1,0:T(8,128)(2,1)S(1)}, u32[]{:S(2)}, u32[]{:S(2)}) collective-permute-start(bf16[2,12,6]{2,1,0:T(8,128)(2,1)S(1)} %get-tuple-element.18), channel_id=1, source_target_pairs={{0,4},{4,8},{8,12},{12,0},{1,5},{5,9},{9,13},{13,1},{2,6},{6,10},{... | collective-permute-start | bytes 872 | tf_op jit(solution)/shard_map/ppermute | solution.py:20
  21.5 24.2 %collective-permute-start.5 = (bf16[2,12,6]{2,1,0:T(8,128)(2,1)S(1)}, bf16[2,12,6]{2,1,0:T(8,128)(2,1)S(1)}, u32[]{:S(2)}, u32[]{:S(2)}) collective-permute-start(bf16[2,12,6]{2,1,0:T(8,128)(2,1)S(1)} %get-tuple-element.19), channel_id=1, source_target_pairs={{4,0},{8,4},{12,8},{0,12},{5,1},{9,5},{13,9},{1,13},{6,2},{10,6},{... | collective-permute-start | bytes 872 | tf_op jit(solution)/shard_map/ppermute | solution.py:23
  45.8 25.9 %collective-permute-start.6 = (bf16[2,3,36]{2,1,0:T(4,128)(2,1)S(1)}, bf16[2,3,36]{2,1,0:T(4,128)(2,1)S(1)}, u32[]{:S(2)}, u32[]{:S(2)}) collective-permute-start(bf16[2,3,36]{2,1,0:T(4,128)(2,1)S(1)} %get-tuple-element.16), channel_id=1, source_target_pairs={{0,2},{1,3},{4,6},{5,7},{8,10},{9,11},{12,14},{13,15},{16,18},{17,... | collective-permute-start | bytes 1304 | tf_op jit(solution)/shard_map/ppermute | solution.py:20
  49.4 22.3 %collective-permute-start.7 = (bf16[2,3,36]{2,1,0:T(4,128)(2,1)S(1)}, bf16[2,3,36]{2,1,0:T(4,128)(2,1)S(1)}, u32[]{:S(2)}, u32[]{:S(2)}) collective-permute-start(bf16[2,3,36]{2,1,0:T(4,128)(2,1)S(1)} %get-tuple-element.17), channel_id=1, source_target_pairs={{2,0},{3,1},{6,4},{7,5},{10,8},{11,9},{14,12},{15,13},{18,16},{19,... | collective-permute-start | bytes 1304 | tf_op jit(solution)/shard_map/ppermute | solution.py:23
  72.3 8.2 %collective-permute-start.2 = (bf16[2,3,36,512]{3,2,1,0:T(8,128)(2,1)S(1)}, bf16[2,3,36,512]{3,2,1,0:T(8,128)(2,1)S(1)}, u32[]{:S(2)}, u32[]{:S(2)}) collective-permute-start(bf16[2,3,36,512]{3,2,1,0:T(8,128)(2,1)S(1)} %get-tuple-element.8), channel_id=1, source_target_pairs={{0,2},{1,3},{4,6},{5,7},{8,10},{9,11},{12,14},{13,15},{16,18},{17,... | collective-permute-start | bytes 663560 | tf_op jit(solution)/shard_map/ppermute | solution.py:20
  76.8 8.1 %collective-permute-start.3 = (bf16[2,3,36,512]{3,2,1,0:T(8,128)(2,1)S(1)}, bf16[2,3,36,512]{3,2,1,0:T(8,128)(2,1)S(1)}, u32[]{:S(2)}, u32[]{:S(2)}) collective-permute-start(bf16[2,3,36,512]{3,2,1,0:T(8,128)(2,1)S(1)} %get-tuple-element.9), channel_id=1, source_target_pairs={{2,0},{3,1},{6,4},{7,5},{10,8},{11,9},{14,12},{15,13},{18,16},{19,... | collective-permute-start | bytes 663560 | tf_op jit(solution)/shard_map/ppermute | solution.py:23
  117.7 9.8 %copy-start.2 = (bf16[1,12,24,512]{3,2,1,0:T(8,128)(2,1)S(1)}, bf16[1,12,24,512]{3,2,1,0:T(8,128)(2,1)}, u32[]{:S(2)}) copy-start(bf16[1,12,24,512]{3,2,1,0:T(8,128)(2,1)} %param.13) | copy-start | bytes 884740
  120.5 46.4 %all-gather.4.cloned.1.call-start = ((), (), s32[]{:S(2)}) async-start(), calls=%async_computation.5 | async-start | bytes 2621440 | tf_op jit(solution)/shard_map/all_gather | solution.py:131
  121.1 9.8 %copy-start.9 = (f32[2048]{0:T(1024)S(1)}, f32[2048]{0:T(1024)}, u32[]{:S(2)}) copy-start(f32[2048]{0:T(1024)} %param.20) | copy-start | bytes 24580
  121.1 76.4 %reduce-scatter.6.cloned.1.call-start = ((), (), s32[]{:S(2)}) async-start(), calls=%async_computation.6 | async-start | bytes 589824 | tf_op jit(solution)/shard_map/reduce_scatter | solution.py:226
  155.7 15.1 %copy-start.13 = (s32[1,6,12]{2,0,1:T(1,128)S(1)}, s32[1,6,12]{2,0,1:T(1,128)}, u32[]{:S(2)}) copy-start(s32[1,6,12]{2,0,1:T(1,128)} %param.15) | copy-start | bytes 868
  170.1 72.5 %all-gather.6.cloned.1.call-start = ((), (), s32[]{:S(2)}) async-start(), calls=%async_computation.7 | async-start | bytes 3932160 | tf_op jit(solution)/shard_map/all_gather | solution.py:110
  170.7 107.5 %all-gather.8.cloned.1.call-start = ((), (), s32[]{:S(2)}) async-start(), calls=%async_computation.8 | async-start | bytes 1310720 | tf_op jit(solution)/shard_map/all_gather | solution.py:124
  172.7 24.7 %collective-permute-start.12 = (bf16[2,6,6]{2,1,0:T(8,128)(2,1)S(1)}, bf16[2,6,6]{2,1,0:T(8,128)(2,1)S(1)}, u32[]{:S(2)}, u32[]{:S(2)}) collective-permute-start(bf16[2,6,6]{2,1,0:T(8,128)(2,1)S(1)} %get-tuple-element.22), channel_id=1, source_target_pairs={{0,4},{4,8},{8,12},{12,0},{1,5},{5,9},{9,13},{13,1},{2,6},{6,10},{... | collective-permute-start | bytes 440 | tf_op jit(solution)/shard_map/ppermute | solution.py:20
  173.0 24.4 %collective-permute-start.13 = (bf16[2,6,6]{2,1,0:T(8,128)(2,1)S(1)}, bf16[2,6,6]{2,1,0:T(8,128)(2,1)S(1)}, u32[]{:S(2)}, u32[]{:S(2)}) collective-permute-start(bf16[2,6,6]{2,1,0:T(8,128)(2,1)S(1)} %get-tuple-element.23), channel_id=1, source_target_pairs={{4,0},{8,4},{12,8},{0,12},{5,1},{9,5},{13,9},{1,13},{6,2},{10,6},{... | collective-permute-start | bytes 440 | tf_op jit(solution)/shard_map/ppermute | solution.py:23
  176.6 110.8 %reduce-scatter.8.cloned.1.call-start = ((), (), s32[]{:S(2)}) async-start(), calls=%async_computation.9 | async-start | bytes 589824 | tf_op jit(solution)/shard_map/reduce_scatter | solution.py:240
  193.3 6.4 %copy-start.11 = (f32[1024]{0:T(1024)S(1)}, f32[1024]{0:T(1024)}, u32[]{:S(2)}) copy-start(f32[1024]{0:T(1024)} %param.22) | copy-start | bytes 12292
  202.9 13.8 %collective-permute-start.8 = (bf16[2,6,6,1024]{3,2,1,0:T(8,128)(2,1)S(1)}, bf16[2,6,6,1024]{3,2,1,0:T(8,128)(2,1)S(1)}, u32[]{:S(2)}, u32[]{:S(2)}) collective-permute-start(bf16[2,6,6,1024]{3,2,1,0:T(8,128)(2,1)S(1)} %get-tuple-element.14), channel_id=1, source_target_pairs={{0,4},{4,8},{8,12},{12,0},{1,5},{5,9},{9,13},{13,1},{2,6},{6,10},{... | collective-permute-start | bytes 442376 | tf_op jit(solution)/shard_map/ppermute | solution.py:20
  203.0 19.8 %collective-permute-start.9 = (bf16[2,6,6,1024]{3,2,1,0:T(8,128)(2,1)S(1)}, bf16[2,6,6,1024]{3,2,1,0:T(8,128)(2,1)S(1)}, u32[]{:S(2)}, u32[]{:S(2)}) collective-permute-start(bf16[2,6,6,1024]{3,2,1,0:T(8,128)(2,1)S(1)} %get-tuple-element.15), channel_id=1, source_target_pairs={{4,0},{8,4},{12,8},{0,12},{5,1},{9,5},{13,9},{1,13},{6,2},{10,6},{... | collective-permute-start | bytes 442376 | tf_op jit(solution)/shard_map/ppermute | solution.py:23
  206.8 21.1 %collective-permute-start.14 = (bf16[2,3,24]{2,1,0:T(4,128)(2,1)S(1)}, bf16[2,3,24]{2,1,0:T(4,128)(2,1)S(1)}, u32[]{:S(2)}, u32[]{:S(2)}) collective-permute-start(bf16[2,3,24]{2,1,0:T(4,128)(2,1)S(1)} %get-tuple-element.20), channel_id=1, source_target_pairs={{0,2},{1,3},{4,6},{5,7},{8,10},{9,11},{12,14},{13,15},{16,18},{17,... | collective-permute-start | bytes 872 | tf_op jit(solution)/shard_map/ppermute | solution.py:20
  210.2 17.7 %collective-permute-start.15 = (bf16[2,3,24]{2,1,0:T(4,128)(2,1)S(1)}, bf16[2,3,24]{2,1,0:T(4,128)(2,1)S(1)}, u32[]{:S(2)}, u32[]{:S(2)}) collective-permute-start(bf16[2,3,24]{2,1,0:T(4,128)(2,1)S(1)} %get-tuple-element.21), channel_id=1, source_target_pairs={{2,0},{3,1},{6,4},{7,5},{10,8},{11,9},{14,12},{15,13},{18,16},{19,... | collective-permute-start | bytes 872 | tf_op jit(solution)/shard_map/ppermute | solution.py:23
  223.2 8.9 %collective-permute-start.10 = (bf16[2,3,24,1024]{3,2,1,0:T(8,128)(2,1)S(1)}, bf16[2,3,24,1024]{3,2,1,0:T(8,128)(2,1)S(1)}, u32[]{:S(2)}, u32[]{:S(2)}) collective-permute-start(bf16[2,3,24,1024]{3,2,1,0:T(8,128)(2,1)S(1)} %get-tuple-element.10), channel_id=1, source_target_pairs={{0,2},{1,3},{4,6},{5,7},{8,10},{9,11},{12,14},{13,15},{16,18},{17,... | collective-permute-start | bytes 884744 | tf_op jit(solution)/shard_map/ppermute | solution.py:20
  226.6 9.7 %collective-permute-start.11 = (bf16[2,3,24,1024]{3,2,1,0:T(8,128)(2,1)S(1)}, bf16[2,3,24,1024]{3,2,1,0:T(8,128)(2,1)S(1)}, u32[]{:S(2)}, u32[]{:S(2)}) collective-permute-start(bf16[2,3,24,1024]{3,2,1,0:T(8,128)(2,1)S(1)} %get-tuple-element.11), channel_id=1, source_target_pairs={{2,0},{3,1},{6,4},{7,5},{10,8},{11,9},{14,12},{15,13},{18,16},{19,... | collective-permute-start | bytes 884744 | tf_op jit(solution)/shard_map/ppermute | solution.py:23
  275.6 11.8 %copy-start.3 = (bf16[1,6,12,1024]{3,2,1,0:T(8,128)(2,1)S(1)}, bf16[1,6,12,1024]{3,2,1,0:T(8,128)(2,1)}, u32[]{:S(2)}) copy-start(bf16[1,6,12,1024]{3,2,1,0:T(8,128)(2,1)} %reduce-scatter.6.cloned.1.call-done) | copy-start | bytes 442372
  275.6 13.4 %copy-start.1 = (f32[32,253]{1,0:T(8,128)S(1)}, f32[32,253]{1,0:T(8,128)}, u32[]{:S(2)}) copy-start(f32[32,253]{1,0:T(8,128)} %param.25) | copy-start | bytes 97156
  (4 other events, 14.2 us)
Sparse Core Ops, SparseCore 0:
  120.6 6.7 reduce-scatter.3
  170.3 6.6 reduce-scatter.5
  280.9 6.4 reduce-scatter.7
Sparse Core Ops, SparseCore 1:
  122.6 44.3 all-gather.3
  172.2 70.4 all-gather.5
  244.1 26.6 all-gather.7
where the time goes:
time: 302 us; the launch traced here: 297 us
  local copies, waits for them, and re-layouts  83.9 us (28%)
  waiting for transfers between devices  57 us (19%)
  blocking collectives  45.2 us (15%)
  starting transfers between devices  37.2 us (12%)
  matrix products  36.1 us (12%)
  other arithmetic  20.9 us (7%)
  between operations  16.6 us (5%)
    all_gather x1, blocking collectives, project_rows(): summed = accumulate(lax.all_gather(inward, 'lon', axis=1, tiled=True))  18.6 us
    ppermute x8, starting transfers between devices, padded(): lax.ppermute(lax.slice_in_dim(block, 0, width, axis=dim), axis, backward)  18.4 us
    ppermute x8, starting transfers between devices, padded(): lax.ppermute(lax.slice_in_dim(block, block.shape[dim] - width, None, axis...  18.1 us
    add x4, local copies, waits for them, and re-layouts, attend(): scores * head_size ** (-0.5) + bias_blocks(bias_table, win_lat, win_lon)  17.6 us
    ppermute x8, waiting for transfers between devices, padded(): lax.ppermute(lax.slice_in_dim(block, 0, width, axis=dim), axis, backward)  14.6 us
    all_gather x1, blocking collectives, output_columns(): return output_project(lax.all_gather(outward, 'lon', axis=0, tiled=True))  14.6 us
    another operation x6, local copies, waits for them, and re-layouts, heads_of(): return blocks.reshape(blocks.shape[:4] + (head_count, head_size))  13.7 us
    ppermute x8, waiting for transfers between devices, padded(): lax.ppermute(lax.slice_in_dim(block, block.shape[dim] - width, None, axis...  11.2 us
  transfers between devices with their start and end apart: 22, of which 10 were waited for; matrix products, arithmetic and copies ran while one was open for 32% of the time, Pallas kernels for 0%

commit v1 on v0

v1 whole, which is shorter than its diff:
```python
import functools

import jax
import jax.numpy as jnp
import numpy as np
from jax import lax
from jax.experimental import pallas as pl
from jax.experimental.pallas import tpu as pltpu
from jax.sharding import PartitionSpec as P

WIN_LAT = 6
WIN_LON = 12
HALF_LAT = WIN_LAT // 2
HALF_LON = WIN_LON // 2
WIN = WIN_LAT * WIN_LON
EPSILON = 1e-05
LANES = 128
MESH = pl.DeviceIdType.MESH
VMEM = pl.BlockSpec(memory_space=pltpu.VMEM)
ANY = pl.BlockSpec(memory_space=pl.ANY)
LIMIT = 60 * 1024 * 1024
NT = (((1,), (1,)), ((), ()))
AROUND = ((0, -1), (0, 1), (-1, 0), (1, 0), (-1, -1), (-1, 1), (1, -1), (1, 1))


def up_to(count, step):
    return -(-count // step) * step


ROWS = up_to(WIN, 16)


class Plan:
    def __init__(self, lat_len, lon_len):
        self.lat_len, self.lon_len = lat_len, lon_len
        self.own = lat_len * lon_len
        self.own_rows = up_to(self.own, 16)
        self.segments = {}
        offset = self.own_rows
        for side in AROUND:
            count = self.extent(side)
            self.segments[side] = (offset, up_to(count, 16))
            offset += up_to(count, 16)
        self.wide_rows = offset
        self.bands = lat_len // WIN_LAT + 1
        self.columns = lon_len // WIN_LON + 1
        self.windows = self.bands * self.columns
        gather = np.full((self.windows * ROWS, 1), -1, np.int32)
        scatter = np.full((self.own_rows, 1), -1, np.int32)
        for w in range(self.windows):
            band, col = divmod(w, self.columns)
            for p in range(WIN):
                r = band * WIN_LAT - HALF_LAT + p // WIN_LON
                c = col * WIN_LON - HALF_LON + p % WIN_LON
                dy = -1 if r < 0 else int(r >= lat_len)
                dx = -1 if c < 0 else int(c >= lon_len)
                if dy == 0 and dx == 0:
                    gather[w * ROWS + p] = r * lon_len + c
                    scatter[r * lon_len + c] = w * ROWS + p
                    continue
                width = HALF_LON if dx else lon_len
                rr = r + HALF_LAT if dy < 0 else (r - lat_len if dy > 0 else r)
                cc = c + HALF_LON if dx < 0 else (c - lon_len if dx > 0 else c)
                gather[w * ROWS + p] = self.segments[(dy, dx)][0] + rr * width + cc
        self.gather, self.scatter = gather, scatter

    def extent(self, side):
        rows = HALF_LAT if side[0] else self.lat_len
        cols = HALF_LON if side[1] else self.lon_len
        return rows * cols

    def edges(self):
        result = np.full((self.wide_rows - self.own_rows, 1), -1, np.int32)
        for dy, dx in AROUND:
            offset = self.segments[(dy, dx)][0] - self.own_rows
            rows = range(self.lat_len)
            rows = rows[-HALF_LAT:] if dy < 0 else (rows[:HALF_LAT] if dy > 0 else rows)
            cols = range(self.lon_len)
            cols = cols[-HALF_LON:] if dx < 0 else (cols[:HALF_LON] if dx > 0 else cols)
            for i, (r, c) in enumerate((r, c) for r in rows for c in cols):
                result[offset + i] = r * self.lon_len + c
        return result

    def patches(self):
        half_lat, half_lon = self.lat_len // 2, self.lon_len // 2
        result = np.full((4, up_to(half_lat * half_lon, 16), 1), -1, np.int32)
        for s in range(2):
            for t in range(2):
                for a in range(half_lat):
                    for b in range(half_lon):
                        result[2 * s + t, a * half_lon + b] = (2 * a + s) * self.lon_len + 2 * b + t
        return result


def onehot(index, width):
    spots = lax.broadcasted_iota(jnp.int32, (index.shape[0], width), 1)
    return jnp.where(spots == index, 1.0, 0.0).astype(jnp.bfloat16)


def pick(index, source):
    return jnp.dot(
        onehot(index, source.shape[0]), source, preferred_element_type=jnp.float32
    ).astype(jnp.bfloat16)


def normalize(values, gain):
    widened = values.astype(jnp.float32)
    center = widened - jnp.mean(widened, axis=-1, keepdims=True)
    spread = jnp.mean(center * center, axis=-1, keepdims=True)
    return (center * lax.rsqrt(spread + EPSILON) * gain).astype(jnp.bfloat16)


def exchange_halo(plan, edge_ref, wide, send_sem, recv_sem):
    lat, lon = lax.axis_index("lat"), lax.axis_index("lon")
    lats, lons = lax.axis_size("lat"), lax.axis_size("lon")

    def place(dy, dx):
        return {"lat": lax.rem(lat + dy + lats, lats), "lon": lax.rem(lon + dx + lons, lons)}

    def when_there(dy, action):
        if dy == 0:
            action()
        else:
            pl.when((lat > 0) if dy < 0 else (lat < lats - 1))(action)

    barrier = pltpu.get_barrier_semaphore()
    for dy, dx in AROUND:
        def greet(dy=dy, dx=dx):
            pl.semaphore_signal(barrier, inc=1, device_id=place(dy, dx), device_id_type=MESH)
        when_there(dy, greet)
    peers = 2 + 3 * (lat > 0).astype(jnp.int32) + 3 * (lat < lats - 1).astype(jnp.int32)
    pl.semaphore_wait(barrier, peers)

    def copy_of(number, dy, dx):
        offset, count = plan.segments[(dy, dx)]
        return pltpu.make_async_remote_copy(
            src_ref=edge_ref.at[pl.ds(offset - plan.own_rows, count)],
            dst_ref=wide.at[pl.ds(offset, count)],
            send_sem=send_sem.at[number],
            recv_sem=recv_sem.at[number],
            device_id=place(-dy, -dx),
            device_id_type=MESH,
        )

    for number, (dy, dx) in enumerate(AROUND):
        when_there(-dy, lambda n=number, y=dy, x=dx: copy_of(n, y, x).start())
        if dy:
            offset, count = plan.segments[(dy, dx)]

            def clear(offset=offset, count=count):
                wide[pl.ds(offset, count), :] = jnp.zeros((count, wide.shape[1]), wide.dtype)

            pl.when(jnp.logical_not((lat > 0) if dy < 0 else (lat < lats - 1)))(clear)

    def finish():
        for number, (dy, dx) in enumerate(AROUND):
            when_there(dy, lambda n=number, y=dy, x=dx: copy_of(n, y, x).wait_recv())
            when_there(-dy, lambda n=number, y=dy, x=dx: copy_of(n, y, x).wait_send())

    return finish


def attend_windows(plan, wide, gather_ref, gain_ref, inward_ref, bias_ref, normed, triple, tags, mixed):
    features = normed.shape[1]
    heads = bias_ref.shape[0]
    size = features // heads
    per_group = LANES // size
    groups = features // LANES
    everything = wide[...]

    for w in range(plan.windows):
        rows = pl.ds(w * ROWS, ROWS)
        chosen = pick(gather_ref[rows, :], everything)
        normed[rows, :] = normalize(chosen[:, :features], gain_ref[...])
        tags[rows, :] = chosen[:, features:]

    step = 256
    for member in range(3):
        @pl.loop(0, features // step)
        def _(block):
            cols = pl.ds(pl.multiple_of(block * step, step), step)
            triple[member, :, cols] = jnp.dot(
                normed[...], inward_ref[member, :, cols], preferred_element_type=jnp.float32
            ).astype(jnp.bfloat16)

    owner = lax.broadcasted_iota(jnp.int32, (ROWS, LANES), 1) // size
    fill = jnp.zeros((LANES - ROWS, LANES), jnp.bfloat16)
    first = jnp.where(
        lax.broadcasted_iota(jnp.int32, (16, LANES), 1) == 0, 1.0, 0.0
    ).astype(jnp.bfloat16)

    def spread(block):
        parts = []
        for h in range(per_group):
            parts += [jnp.where(owner == h, block, jnp.zeros_like(block)), fill]
        return jnp.concatenate(parts, axis=0)

    @pl.loop(0, plan.windows)
    def _(w):
        rows = pl.ds(pl.multiple_of(w * ROWS, ROWS), ROWS)
        tag_block = tags[rows, :]
        across = lax.dot_general(
            first, jnp.concatenate([tag_block, fill], axis=0), NT, preferred_element_type=jnp.float32
        )
        allowed = tag_block[:, :1].astype(jnp.float32) == across[:1, :]

        @pl.loop(0, groups, unroll=2)
        def _(g):
            cols = pl.ds(pl.multiple_of(g * LANES, LANES), LANES)
            keys = spread(triple[1, rows, cols])
            scores = lax.dot_general(
                triple[0, rows, cols], keys, NT, preferred_element_type=jnp.float32
            )
            shares = []
            for h in range(per_group):
                score = scores[:, h * LANES : (h + 1) * LANES] * size ** (-0.5)
                score = score + bias_ref[g * per_group + h]
                score = jnp.where(allowed, score, -1e30)
                weight = jnp.exp(score - jnp.max(score, axis=-1, keepdims=True))
                total = jnp.sum(weight, axis=-1, keepdims=True)
                shares.append((weight * (1.0 / total)).astype(jnp.bfloat16))
            blended = jnp.dot(
                jnp.concatenate(shares, axis=1),
                spread(triple[2, rows, cols]),
                preferred_element_type=jnp.float32,
            )
            mixed[rows, cols] = blended.astype(jnp.bfloat16)


def fine_kernel(
    plan, own_ref, edge_ref, tag_ref, gather_ref, scatter_ref, patch_ref, edge_index_ref, gain_ref,
    inward_ref, outward_ref, bias_ref, merge_gain_ref, merge_ref,
    fine_ref, coarse_ref, coarse_edge_ref, wide, normed, triple, tags, mixed, send_sem, recv_sem,
):
    features = normed.shape[1]
    finish = exchange_halo(plan, edge_ref, wide, send_sem, recv_sem)
    wide[: plan.own_rows, :] = own_ref[...]
    finish()
    attend_windows(plan, wide, gather_ref, gain_ref, inward_ref, bias_ref, normed, triple, tags, mixed)
    own_mixed = pick(scatter_ref[...], mixed[...])
    update = lax.dot_general(own_mixed, outward_ref[0], NT, preferred_element_type=jnp.float32)
    fine = (own_ref[:, :features].astype(jnp.float32) + update).astype(jnp.bfloat16)
    fine_ref[...] = fine
    members = [pick(patch_ref[m], fine).astype(jnp.float32) for m in range(4)]
    count = 4 * features
    mean = sum(jnp.sum(m, axis=-1, keepdims=True) for m in members) / count
    centers = [m - mean for m in members]
    spread = sum(jnp.sum(c * c, axis=-1, keepdims=True) for c in centers) / count
    factor = lax.rsqrt(spread + EPSILON)
    merged = None
    for m in range(4):
        cols = slice(m * features, (m + 1) * features)
        part = (centers[m] * factor * merge_gain_ref[:, cols]).astype(jnp.bfloat16)
        term = lax.dot_general(part, merge_ref[0, :, cols], NT, preferred_element_type=jnp.float32)
        merged = term if merged is None else merged + term
    coarse = jnp.concatenate([merged.astype(jnp.bfloat16), tag_ref[...]], axis=1)
    coarse_ref[...] = coarse
    coarse_edge_ref[...] = pick(edge_index_ref[...], coarse)


def coarse_kernel(
    plan, own_ref, edge_ref, gather_ref, scatter_ref, gain_ref, inward_ref, outward_ref, bias_ref,
    out_ref, wide, normed, triple, tags, mixed, send_sem, recv_sem,
):
    features = normed.shape[1]
    finish = exchange_halo(plan, edge_ref, wide, send_sem, recv_sem)
    wide[: plan.own_rows, :] = own_ref[...]
    finish()
    attend_windows(plan, wide, gather_ref, gain_ref, inward_ref, bias_ref, normed, triple, tags, mixed)
    own_mixed = pick(scatter_ref[...], mixed[...])
    update = lax.dot_general(own_mixed, outward_ref[0], NT, preferred_element_type=jnp.float32)
    out_ref[...] = (own_ref[:, :features].astype(jnp.float32) + update).astype(jnp.bfloat16)


def level_scratch(plan, features):
    rows = plan.windows * ROWS
    return [
        pltpu.VMEM((plan.wide_rows, features + LANES), jnp.bfloat16),
        pltpu.VMEM((rows, features), jnp.bfloat16),
        pltpu.VMEM((3, rows, features), jnp.bfloat16),
        pltpu.VMEM((rows, LANES), jnp.bfloat16),
        pltpu.VMEM((rows, features), jnp.bfloat16),
        pltpu.SemaphoreType.DMA((len(AROUND),)),
        pltpu.SemaphoreType.DMA((len(AROUND),)),
    ]


def gather_kernel(count, split, *refs):
    shards, fulls = refs[:count], refs[count : 2 * count]
    (local_sem, lon_send, lon_recv, one_send, one_recv, two_send, two_recv, lvl_send, lvl_recv) = refs[2 * count :]
    grp, lat, lon, lvl = (lax.axis_index(a) for a in ("grp", "lat", "lon", "lvl"))
    grps, lats, lons, lvls = (lax.axis_size(a) for a in ("grp", "lat", "lon", "lvl"))
    halves = 2 if split else 1

    def at(axis, index, size, step):
        return {axis: lax.rem(index + step, size)}

    greeted = [at("lon", lon, lons, d) for d in range(1, lons)]
    if split:
        greeted += [at("lat", lat, lats, d) for d in range(1, lats)]
        greeted += [at("grp", grp, grps, d) for d in range(1, grps)]
    greeted += [at("lvl", lvl, lvls, d) for d in range(1, lvls)]
    barrier = pltpu.get_barrier_semaphore()
    for device in greeted:
        pl.semaphore_signal(barrier, inc=1, device_id=device, device_id_type=MESH)
    pl.semaphore_wait(barrier, len(greeted))

    def place(m, lon_of, lvl_of, start, size):
        rows, cols = shards[m].shape[1:]
        return fulls[m].at[
            :, pl.ds(pl.multiple_of(lon_of * rows + start, 16), size), pl.ds(pl.multiple_of(lvl_of * cols, cols), cols)
        ]

    def remote(src, dst, send, recv, device):
        return pltpu.make_async_remote_copy(
            src_ref=src, dst_ref=dst, send_sem=send, recv_sem=recv, device_id=device, device_id_type=MESH
        )

    def piece(m, half, grp_of, lat_of):
        rows = shards[m].shape[1]
        if not split:
            return 0, rows
        size = rows // (2 * grps * lats)
        order = grp_of * lats + lat_of if half == 0 else lat_of * grps + grp_of
        return half * (rows // 2) + order * size, size

    def own_copy(m):
        rows = shards[m].shape[1]
        return pltpu.make_async_copy(shards[m], place(m, lon, lvl, 0, rows), local_sem.at[m])

    def lon_copy(m, d, half):
        start, size = piece(m, half, grp, lat)
        return remote(
            shards[m].at[:, pl.ds(start if isinstance(start, int) else pl.multiple_of(start, 16), size), :],
            place(m, lon, lvl, start, size),
            lon_send.at[m, d - 1, half], lon_recv.at[m, d - 1, half], at("lon", lon, lons, d),
        )

    def plane(half, first):
        by_lat = (half == 0) == first
        return ("lat", lat, lats) if by_lat else ("grp", grp, grps)

    def one_copy(m, d, half, e):
        source = lax.rem(lon - d + lons, lons)
        start, size = piece(m, half, grp, lat)
        block = place(m, source, lvl, start, size)
        return remote(block, block, one_send.at[m, d - 1, half, e - 1], one_recv.at[m, d - 1, half, e - 1], at(*plane(half, True), e))

    def two_copy(m, d, half, e):
        source = lax.rem(lon - d + lons, lons)
        if half == 0:
            start, size = piece(m, half, grp, 0)
            size *= lats
        else:
            start, size = piece(m, half, 0, lat)
            size *= grps
        block = place(m, source, lvl, start, size)
        return remote(block, block, two_send.at[m, d - 1, half, e - 1], two_recv.at[m, d - 1, half, e - 1], at(*plane(half, False), e))

    def lvl_copy(m, d, e):
        rows = shards[m].shape[1]
        source = lax.rem(lon - d + lons, lons)
        block = place(m, source, lvl, 0, rows)
        return remote(
            shards[m] if d == 0 else block, block,
            lvl_send.at[m, d, e - 1], lvl_recv.at[m, d, e - 1], at("lvl", lvl, lvls, e),
        )

    ways = [(d, half) for d in range(1, lons) for half in range(halves)]
    for m in range(count):
        own_copy(m).start()
        for d, half in ways:
            lon_copy(m, d, half).start()
        for e in range(1, lvls):
            lvl_copy(m, 0, e).start()

    def others(half, first):
        return range(1, plane(half, first)[2])

    def share_one(m):
        for d, half in ways:
            lon_copy(m, d, half).wait_recv()
            if split:
                for e in others(half, True):
                    one_copy(m, d, half, e).start()

    def share_two(m):
        for d, half in ways:
            if split:
                for e in others(half, True):
                    one_copy(m, d, half, e).wait_recv()
                for e in others(half, False):
                    two_copy(m, d, half, e).start()

    def share_lvl(m):
        for d in range(1, lons):
            if split:
                for half in range(halves):
                    for e in others(half, False):
                        two_copy(m, d, half, e).wait_recv()
            for e in range(1, lvls):
                lvl_copy(m, d, e).start()

    for s in range(count + 2):
        if s < count:
            share_one(s)
        if 0 <= s - 1 < count:
            share_two(s - 1)
        if 0 <= s - 2 < count:
            share_lvl(s - 2)
    for m in range(count):
        own_copy(m).wait()
        for d in range(lons):
            for e in range(1, lvls):
                lvl_copy(m, d, e).wait()
        for d, half in ways:
            lon_copy(m, d, half).wait_send()
            if split:
                for e in others(half, True):
                    one_copy(m, d, half, e).wait_send()
                for e in others(half, False):
                    two_copy(m, d, half, e).wait_send()


def gather_weights(weights):
    grps, lats, lons, lvls = (lax.axis_size(a) for a in ("grp", "lat", "lon", "lvl"))
    split = all(w.shape[1] % (2 * grps * lats * 16) == 0 for w in weights)
    count = len(weights)
    halves = 2 if split else 1
    dma = pltpu.SemaphoreType.DMA
    most = max(grps, lats) - 1 if split else 1
    return pl.pallas_call(
        functools.partial(gather_kernel, count, split),
        out_shape=[
            jax.ShapeDtypeStruct((w.shape[0], w.shape[1] * lons, w.shape[2] * lvls), w.dtype) for w in weights
        ],
        in_specs=[ANY] * count,
        out_specs=[VMEM] * count,
        scratch_shapes=[dma((count,))]
        + [dma((count, lons - 1, halves))] * 2
        + [dma((count, lons - 1, halves, most))] * 4
        + [dma((count, lons, lvls - 1))] * 2,
        compiler_params=pltpu.CompilerParams(collective_id=0, has_side_effects=True, vmem_limit_bytes=LIMIT),
        name="gather_weights",
    )(*weights)


def bias_blocks(table):
    span_lon = 2 * WIN_LON - 1
    p = np.arange(WIN)
    r, c = p // WIN_LON, p % WIN_LON
    number = (r[:, None] - r[None, :] + WIN_LAT - 1) * span_lon + c[:, None] - c[None, :] + WIN_LON - 1
    lat_hot = (r[:, None] - r[None, :] + WIN_LAT - 1)[:, :, None]
    del number
    heads = table.shape[0]
    grid = table.reshape(heads, 2 * WIN_LAT - 1, span_lon)
    i, j = np.arange(WIN_LON)[:, None], np.arange(WIN_LON)[None, :]
    lon_blocks = jnp.stack(
        [lax.slice_in_dim(grid, k, k + WIN_LON, axis=2)[:, :, ::-1] for k in range(WIN_LON)], axis=2
    )
    del lat_hot, i, j
    rows = []
    for k in range(WIN_LAT):
        parts = [lon_blocks[:, k - l + WIN_LAT - 1] for l in range(WIN_LAT)]
        rows.append(jnp.concatenate(parts, axis=2))
    blocks = jnp.concatenate(rows, axis=1)
    return jnp.pad(blocks, ((0, 0), (0, ROWS - WIN), (0, LANES - WIN)))


def shards(
    tokens, fine_tags, coarse_tags, fine_gain, fine_inward, fine_outward, fine_table, merge_gain,
    merge_weight, coarse_gain, coarse_inward, coarse_outward, coarse_table,
):
    _, lat_len, lon_len, width = tokens.shape
    fine_plan, coarse_plan = Plan(lat_len, lon_len), Plan(lat_len // 2, lon_len // 2)
    inward, outward, merge, inward_two, outward_two = gather_weights(
        [fine_inward, fine_outward[None], merge_weight[None], coarse_inward, coarse_outward[None]]
    )
    fine_bias, coarse_bias = bias_blocks(fine_table), bias_blocks(coarse_table)

    tagged = jnp.concatenate(
        [tokens[0], jnp.broadcast_to(fine_tags[0, :, :, None], (lat_len, lon_len, LANES)).astype(jnp.bfloat16)], axis=2
    )
    own = tagged.reshape(lat_len * lon_len, -1)
    own = jnp.pad(own, ((0, fine_plan.own_rows - fine_plan.own), (0, 0)))
    pieces = []
    for dy, dx in AROUND:
        part = tagged
        part = part[-HALF_LAT:] if dy < 0 else (part[:HALF_LAT] if dy > 0 else part)
        part = part[:, -HALF_LON:] if dx < 0 else (part[:, :HALF_LON] if dx > 0 else part)
        part = part.reshape(-1, part.shape[2])
        pieces.append(jnp.pad(part, ((0, up_to(part.shape[0], 16) - part.shape[0]), (0, 0))))
    edge = jnp.concatenate(pieces, axis=0)
    coarse_width = merge.shape[1]
    coarse_marks = jnp.broadcast_to(coarse_tags.reshape(-1, 1), (coarse_plan.own, LANES)).astype(jnp.bfloat16)
    coarse_marks = jnp.pad(coarse_marks, ((0, coarse_plan.own_rows - coarse_plan.own), (0, 0)))

    edge_rows = coarse_plan.wide_rows - coarse_plan.own_rows
    fine, coarse_own, coarse_edge = pl.pallas_call(
        functools.partial(fine_kernel, fine_plan),
        out_shape=[
            jax.ShapeDtypeStruct((fine_plan.own_rows, width), jnp.bfloat16),
            jax.ShapeDtypeStruct((coarse_plan.own_rows, coarse_width + LANES), jnp.bfloat16),
            jax.ShapeDtypeStruct((edge_rows, coarse_width + LANES), jnp.bfloat16),
        ],
        in_specs=[VMEM] * 13,
        out_specs=[VMEM] * 3,
        scratch_shapes=level_scratch(fine_plan, width),
        compiler_params=pltpu.CompilerParams(collective_id=1, has_side_effects=True, vmem_limit_bytes=LIMIT),
        name="fine_level",
    )(
        own, edge, coarse_marks, fine_plan.gather, fine_plan.scatter, fine_plan.patches(),
        coarse_plan.edges(), fine_gain[None], inward, outward, fine_bias, merge_gain[None], merge,
    )
    coarse = pl.pallas_call(
        functools.partial(coarse_kernel, coarse_plan),
        out_shape=jax.ShapeDtypeStruct((coarse_plan.own_rows, coarse_width), jnp.bfloat16),
        in_specs=[VMEM] * 8,
        out_specs=VMEM,
        scratch_shapes=level_scratch(coarse_plan, coarse_width),
        compiler_params=pltpu.CompilerParams(collective_id=2, has_side_effects=True, vmem_limit_bytes=LIMIT),
        name="coarse_level",
    )(
        coarse_own, coarse_edge, coarse_plan.gather, coarse_plan.scatter, coarse_gain[None],
        inward_two, outward_two, coarse_bias,
    )
    fine = fine[: fine_plan.own].reshape(tokens.shape)
    coarse = coarse[: coarse_plan.own].reshape(1, lat_len // 2, lon_len // 2, coarse_width)
    return fine, coarse


def solution(mesh):
    placed = (
        P(("grp", "lvl"), "lat", "lon", None),
        P(("grp", "lvl"), "lat", "lon"),
        P(("grp", "lvl"), "lat", "lon"),
        P(),
        P(None, "lon", "lvl"),
        P("lon", "lvl"),
        P(),
        P(),
        P("lon", "lvl"),
        P(),
        P(None, "lon", "lvl"),
        P("lon", "lvl"),
        P(),
    )
    return jax.shard_map(
        shards,
        mesh=mesh,
        in_specs=placed,
        out_specs=(P(("grp", "lvl"), "lat", "lon", None), P(("grp", "lvl"), "lat", "lon", None)),
        check_vma=False,
    )
```

time: 302 us -> 210 us (0.70); the launches traced: 297 us -> 209 us
  Pallas kernels: 0 us -> 162 us
  waiting for transfers between devices: 57 us -> 0 us
  blocking collectives: 45.2 us -> 0 us
  local copies, waits for them, and re-layouts: 83.9 us -> 42 us
  starting transfers between devices: 37.2 us -> 0 us
  matrix products: 36.1 us -> 0 us
  other arithmetic: 20.9 us -> 4.24 us
  between operations: 16.6 us -> 1.32 us
    pallas_call x0 -> x3, Pallas kernels: none -> 162 us  [the longest x1 80.1 us: gather_weights(): pl.pallas_call(functools.partial(gather_kernel, count, split), out_shape=...]
    all_gather x6 -> x0, blocking collectives: 41.2 us -> none  [the longest x1 18.6 us: project_rows(): summed = accumulate(lax.all_gather(inward, 'lon', axis=1, tiled=True))]
    ppermute x16 -> x0, starting transfers between devices: 36.5 us -> none  [the longest x8 18.4 us: padded(): lax.ppermute(lax.slice_in_dim(block, 0, width, axis=dim), axis, backward)]
    dot_general x13 -> x0, matrix products: 36.1 us -> none  [the longest x2 9.12 us: attend(): jnp.einsum('zabphd,zabqhd->zabhpq', query_heads, key_heads, preferred_ele...]
    ppermute x16 -> x0, waiting for transfers between devices: 25.8 us -> none  [the longest x8 14.6 us: padded(): lax.ppermute(lax.slice_in_dim(block, 0, width, axis=dim), axis, backward)]
    add x4 -> x0, local copies, waits for them, and re-layouts: 17.6 us -> none  [attend(): scores * head_size ** (-0.5) + bias_blocks(bias_table, win_lat, win_lon)]
    all_gather x3 -> x0, waiting for transfers between devices: 17.3 us -> none  [the longest x1 11.2 us: merge_columns(): lax.all_gather(merge_rows, 'lon', axis=0, tiled=True)]
    reduce_scatter x3 -> x0, waiting for transfers between devices: 12.9 us -> none  [the longest x1 6.64 us: shards(): lax.psum_scatter(partial_coarse.reshape(coarse_all.shape[:3] + (-1,)).ast...]
  transfers between devices with their start and end apart: 22 -> 0, of which waited for: 10 -> 0; matrix products, arithmetic and copies ran while one was open for 32% -> 0% of each run, Pallas kernels for 0% -> 0%
where the time goes in v1:
time: 210 us; the launch traced here: 209 us
  Pallas kernels  162 us (77%)
  local copies, waits for them, and re-layouts  42 us (20%)
  other arithmetic  4.24 us (2%)
    pallas_call x1, Pallas kernels, gather_weights(): pl.pallas_call(functools.partial(gather_kernel, count, split), out_shape=...  80.1 us
    pallas_call x1, Pallas kernels, shards(): pl.pallas_call(functools.partial(fine_kernel, fine_plan), out_shape=[jax....  43.4 us
    pallas_call x1, Pallas kernels, shards(): pl.pallas_call(functools.partial(coarse_kernel, coarse_plan), out_shape=j...  38.2 us
    another operation x2, local copies, waits for them, and re-layouts, bias_blocks(): jnp.stack([lax.slice_in_dim(grid, k, k + WIN_LON, axis=2)[:, :, ::-1] for...  12.5 us
    rev x24, local copies, waits for them, and re-layouts, bias_blocks(): lax.slice_in_dim(grid, k, k + WIN_LON, axis=2)[:, :, ::-1]  9.05 us
    concatenate x12, local copies, waits for them, and re-layouts, bias_blocks(): rows.append(jnp.concatenate(parts, axis=2))  7.34 us

profile of v1, /device:TPU:0, one launch (start us, length us, event | category | flops | bytes accessed | tf_op | source)
XLA Modules:
  0.0 209.2 jit_solution(3636598205505753936)
XLA Ops:
  0.6 0.8 convert_reduce_fusion.1
  1.6 1.7 pad_maximum_fusion.own_ref
  3.4 0.7 convert_element_type.34
  4.2 1.0 fusion.1
  5.7 0.7 pad.49.tag_ref
  6.4 80.1 %gather_weights.1 = (bf16[3,512,512]{2,1,0:T(8,128)(2,1)}, bf16[1,512,512]{2,1,0:T(8,128)(2,1)}, bf16[1,1024,2048]{2,1,0:T(8,128)(2,1)}, bf16[3,1024,1024]{2,1,0:T(8,128)(2,1)}, bf16[1,1024,1024]{2,1,0:T(8,128)(2,1)}) custom-call(bf16[3,128,256]{2,1,0:T(8,128)(2,1)} %refs_0_.1, bf16[1,128,256]{2,1,0:T(8,128)(2,1)} %bitcast.115, ...), custom_call_target="tpu_custom_call" | custom-call | tf_op jit(solution)/shard_map/gather_weights/pallas_call | solution.py:432
  88.6 4.5 %stack.90 = f32[16,11,12,12]{3,2,0,1:T(8,128)S(1)} concatenate(f32[16,11,1,12]{3,2,0,1:T(1,128)S(1)} %bitcast.101, f32[16,11,1,12]{3,2,0,1:T(1,128)S(1)} %bitcast.102, f32[16,11,1,12]{3,2,0,1:T(1,128)S(1)} %bitcast.103, f32[16,11,1,12]{3,2,0,1:T(1,128)S(1)} %bitcast.104, f32[16,11,1,12]{3,2,0,1:T(1,128)S(1)} %bitcast.105, f32[16,11,1,12]{3,2,0,1:T(1,128)S(1)} %bitcast.106, ...), dimensions={2} | concatenate | bytes 202752 | tf_op jit(solution)/shard_map/stack | solution.py:458
  94.7 0.5 concatenate.63
  95.3 0.9 pad.50.bias_ref
  96.2 43.4 %fine_level.1 = (bf16[288,512]{1,0:T(8,128)(2,1)}, bf16[80,1152]{1,0:T(8,128)(2,1)}, bf16[320,1152]{1,0:T(8,128)(2,1)}) custom-call(bf16[288,640]{1,0:T(8,128)(2,1)} %pad_maximum_fusion.own_ref, bf16[448,640]{1,0:T(8,128)(2,1)} %copy-done.8, bf16[80,128]{1,0:T(8,128)(2,1)} %pad.49.tag_ref, s32[720,1]{1,0:T(8,128)} %constant.17.clone.gather_ref, ...), custom_call_target="tpu_custom_call" | custom-call | tf_op jit(solution)/shard_map/fine_level/pallas_call | solution.py:499
  139.7 0.8 fusion.7
  140.8 0.8 rev.85
  141.6 0.8 rev.86
  142.5 0.8 rev.87
  143.3 0.8 rev.88
  144.2 0.8 rev.89
  145.1 0.8 rev.90
  145.9 0.8 rev.91
  146.8 0.8 rev.92
  147.6 0.8 rev.93
  148.5 0.8 rev.94
  149.4 8.0 %stack.103 = f32[32,11,12,12]{3,2,0,1:T(8,128)S(1)} concatenate(f32[32,11,1,12]{3,2,0,1:T(1,128)S(1)} %bitcast.86, f32[32,11,1,12]{3,2,0,1:T(1,128)} %bitcast.87, f32[32,11,1,12]{3,2,0,1:T(1,128)} %bitcast.88, f32[32,11,1,12]{3,2,0,1:T(1,128)} %bitcast.89, f32[32,11,1,12]{3,2,0,1:T(1,128)} %bitcast.90, f32[32,11,1,12]{3,2,0,1:T(1,128)} %bitcast.91, f32[32,11,1,12]{3,2,0,1:T(1,128)} %bitcast.92, ...), dimensions={2} | concatenate | bytes 405504 | tf_op jit(solution)/shard_map/stack | solution.py:458
  157.4 1.4 slice_bitcast_fusion
  158.9 1.8 concatenate.64
  160.7 1.7 concatenate.65
  163.8 1.1 concatenate.69
  164.9 2.6 %concatenate.70 = f32[32,72,72]{2,1,0:T(8,128)S(1)} concatenate(f32[32,12,72]{2,1,0:T(8,128)S(1)} %concatenate.64, f32[32,12,72]{2,1,0:T(8,128)S(1)} %concatenate.65, f32[32,12,72]{2,1,0:T(8,128)S(1)} %concatenate.66, f32[32,12,72]{2,1,0:T(8,128)S(1)} %concatenate.67, f32[32,12,72]{2,1,0:T(8,128)S(1)} %concatenate.68, f32[32,12,72]{2,1,0:T(8,128)} %concatenate.69), dimensions={1} | concatenate | bytes 1327104 | tf_op jit(solution)/shard_map/concatenate | solution.py:466
  167.5 1.1 pad.51.bias_ref
  168.7 38.2 %coarse_level.1 = bf16[80,1024]{1,0:T(8,128)(2,1)} custom-call(bf16[80,1152]{1,0:T(8,128)(2,1)} %get-tuple-element.14.own_ref, bf16[320,1152]{1,0:T(8,128)(2,1)} %get-tuple-element.15.edge_ref, s32[320,1]{1,0:T(8,128)} %constant.21.clone.gather_ref, s32[80,1]{1,0:T(8,128)} %constant.22.clone.scatter_ref, f32[1,1024]{1,0:T(1,128)} %bitcast.118, ...), custom_call_target="tpu_custom_call" | custom-call | tf_op jit(solution)/shard_map/coarse_level/pallas_call | solution.py:515
  206.9 0.9 slice.277
  207.8 0.7 reshape.63
  208.5 0.7 copy.166
  (100 shorter events, 6.7 us)
Async XLA Ops:
  0.6 4.7 %copy-start.3 = (bf16[1,12,24,512]{3,2,1,0:T(8,128)(2,1)S(1)}, bf16[1,12,24,512]{3,2,1,0:T(8,128)(2,1)}, u32[]{:S(2)}) copy-start(bf16[1,12,24,512]{3,2,1,0:T(8,128)(2,1)} %param.19) | copy-start | bytes 884740
  1.6 4.0 %copy-start.12 = (s32[1,6,12]{2,0,1:T(1,128)S(1)}, s32[1,6,12]{2,0,1:T(1,128)}, u32[]{:S(2)}) copy-start(s32[1,6,12]{2,0,1:T(1,128)} %param.21) | copy-start | bytes 868
  5.2 81.3 %copy-start.11 = (f32[16,253]{1,0:T(8,128)S(1)}, f32[16,253]{1,0:T(8,128)}, u32[]{:S(2)}) copy-start(f32[16,253]{1,0:T(8,128)} %param.25) | copy-start | bytes 48580
  5.6 81.5 %copy-start.8 = (bf16[448,640]{1,0:T(8,128)(2,1)}, bf16[448,640]{1,0:T(8,128)(2,1)S(1)}, u32[]{:S(2)}) copy-start(bf16[448,640]{1,0:T(8,128)(2,1)S(1)} %pad_dynamic-update-slice_fusion.4.edge_ref) | copy-start | bytes 1720324
  96.2 43.4 %copy-start.10 = (f32[32,253]{1,0:T(8,128)S(1)}, f32[32,253]{1,0:T(8,128)}, u32[]{:S(2)}) copy-start(f32[32,253]{1,0:T(8,128)} %param.31) | copy-start | bytes 97156
  158.8 3.5 %copy-start = (f32[32,12,12]{2,1,0:T(8,128)S(1)}, f32[32,12,12]{2,1,0:T(8,128)}, u32[]{:S(2)}) copy-start(f32[32,12,12]{2,1,0:T(8,128)} %get-tuple-element.27) | copy-start | bytes 55300
  158.8 3.5 %copy-start.1 = (f32[32,12,12]{2,1,0:T(8,128)S(1)}, f32[32,12,12]{2,1,0:T(8,128)}, u32[]{:S(2)}) copy-start(f32[32,12,12]{2,1,0:T(8,128)} %get-tuple-element.21) | copy-start | bytes 55300
  158.8 3.5 %copy-start.2 = (f32[32,12,12]{2,1,0:T(8,128)S(1)}, f32[32,12,12]{2,1,0:T(8,128)}, u32[]{:S(2)}) copy-start(f32[32,12,12]{2,1,0:T(8,128)} %get-tuple-element.26) | copy-start | bytes 55300
  158.8 3.5 %copy-start.5 = (f32[32,12,12]{2,1,0:T(8,128)S(1)}, f32[32,12,12]{2,1,0:T(8,128)}, u32[]{:S(2)}) copy-start(f32[32,12,12]{2,1,0:T(8,128)} %get-tuple-element.25) | copy-start | bytes 55300
  160.6 2.2 %copy-start.4 = (f32[32,12,12]{2,1,0:T(8,128)S(1)}, f32[32,12,12]{2,1,0:T(8,128)}, u32[]{:S(2)}) copy-start(f32[32,12,12]{2,1,0:T(8,128)} %get-tuple-element.20) | copy-start | bytes 55300
  162.3 1.0 copy-start.6
  162.8 1.0 copy-start.7
  168.7 39.9 %copy-start.9 = (bf16[288,512]{1,0:T(8,128)(2,1)S(1)}, bf16[288,512]{1,0:T(8,128)(2,1)}, u32[]{:S(2)}) copy-start(bf16[288,512]{1,0:T(8,128)(2,1)} %get-tuple-element.13) | copy-start | bytes 884740

commit v2 on v1

v2 whole, which is shorter than its diff:
```python
import functools

import jax
import jax.numpy as jnp
import numpy as np
from jax import lax
from jax.experimental import pallas as pl
from jax.experimental.pallas import tpu as pltpu
from jax.sharding import PartitionSpec as P

WIN_LAT = 6
WIN_LON = 12
HALF_LAT = WIN_LAT // 2
HALF_LON = WIN_LON // 2
WIN = WIN_LAT * WIN_LON
EPSILON = 1e-05
LANES = 128
MESH = pl.DeviceIdType.MESH
VMEM = pl.BlockSpec(memory_space=pltpu.VMEM)
ANY = pl.BlockSpec(memory_space=pl.ANY)
LIMIT = 60 * 1024 * 1024
NT = (((1,), (1,)), ((), ()))
AROUND = ((0, -1), (0, 1), (-1, 0), (1, 0), (-1, -1), (-1, 1), (1, -1), (1, 1))


def up_to(count, step):
    return -(-count // step) * step


ROWS = up_to(WIN, 16)


class Plan:
    def __init__(self, lat_len, lon_len):
        self.lat_len, self.lon_len = lat_len, lon_len
        self.own = lat_len * lon_len
        self.own_rows = up_to(self.own, 16)
        self.segments = {}
        offset = self.own_rows
        for side in AROUND:
            count = self.extent(side)
            self.segments[side] = (offset, up_to(count, 16))
            offset += up_to(count, 16)
        self.wide_rows = offset
        self.bands = lat_len // WIN_LAT + 1
        self.columns = lon_len // WIN_LON + 1
        self.windows = self.bands * self.columns
        gather = np.full((self.windows * ROWS, 1), -1, np.int32)
        scatter = np.full((self.own_rows, 1), -1, np.int32)
        for w in range(self.windows):
            band, col = divmod(w, self.columns)
            for p in range(WIN):
                r = band * WIN_LAT - HALF_LAT + p // WIN_LON
                c = col * WIN_LON - HALF_LON + p % WIN_LON
                dy = -1 if r < 0 else int(r >= lat_len)
                dx = -1 if c < 0 else int(c >= lon_len)
                if dy == 0 and dx == 0:
                    gather[w * ROWS + p] = r * lon_len + c
                    scatter[r * lon_len + c] = w * ROWS + p
                    continue
                width = HALF_LON if dx else lon_len
                rr = r + HALF_LAT if dy < 0 else (r - lat_len if dy > 0 else r)
                cc = c + HALF_LON if dx < 0 else (c - lon_len if dx > 0 else c)
                gather[w * ROWS + p] = self.segments[(dy, dx)][0] + rr * width + cc
        self.gather, self.scatter = gather, scatter

    def extent(self, side):
        rows = HALF_LAT if side[0] else self.lat_len
        cols = HALF_LON if side[1] else self.lon_len
        return rows * cols

    def edges(self):
        result = np.full((self.wide_rows - self.own_rows, 1), -1, np.int32)
        for dy, dx in AROUND:
            offset = self.segments[(dy, dx)][0] - self.own_rows
            rows = range(self.lat_len)
            rows = rows[-HALF_LAT:] if dy < 0 else (rows[:HALF_LAT] if dy > 0 else rows)
            cols = range(self.lon_len)
            cols = cols[-HALF_LON:] if dx < 0 else (cols[:HALF_LON] if dx > 0 else cols)
            for i, (r, c) in enumerate((r, c) for r in rows for c in cols):
                result[offset + i] = r * self.lon_len + c
        return result

    def patches(self):
        half_lat, half_lon = self.lat_len // 2, self.lon_len // 2
        result = np.full((4, up_to(half_lat * half_lon, 16), 1), -1, np.int32)
        for s in range(2):
            for t in range(2):
                for a in range(half_lat):
                    for b in range(half_lon):
                        result[2 * s + t, a * half_lon + b] = (2 * a + s) * self.lon_len + 2 * b + t
        return result


def onehot(index, width):
    spots = lax.broadcasted_iota(jnp.int32, (index.shape[0], width), 1)
    return jnp.where(spots == index, 1.0, 0.0).astype(jnp.bfloat16)


def pick(index, source):
    return jnp.dot(
        onehot(index, source.shape[0]), source, preferred_element_type=jnp.float32
    ).astype(jnp.bfloat16)


def normalize(values, gain):
    widened = values.astype(jnp.float32)
    center = widened - jnp.mean(widened, axis=-1, keepdims=True)
    spread = jnp.mean(center * center, axis=-1, keepdims=True)
    return (center * lax.rsqrt(spread + EPSILON) * gain).astype(jnp.bfloat16)


def exchange_halo(plan, edge_ref, wide, send_sem, recv_sem, greeted=()):
    lat, lon = lax.axis_index("lat"), lax.axis_index("lon")
    lats, lons = lax.axis_size("lat"), lax.axis_size("lon")

    def place(dy, dx):
        return {"lat": lax.rem(lat + dy + lats, lats), "lon": lax.rem(lon + dx + lons, lons)}

    def when_there(dy, action):
        if dy == 0:
            action()
        else:
            pl.when((lat > 0) if dy < 0 else (lat < lats - 1))(action)

    barrier = pltpu.get_barrier_semaphore()
    for dy, dx in AROUND:
        def greet(dy=dy, dx=dx):
            pl.semaphore_signal(barrier, inc=1, device_id=place(dy, dx), device_id_type=MESH)
        when_there(dy, greet)
    peers = 2 + 3 * (lat > 0).astype(jnp.int32) + 3 * (lat < lats - 1).astype(jnp.int32)
    for device in greeted:
        pl.semaphore_signal(barrier, inc=1, device_id=device, device_id_type=MESH)
    pl.semaphore_wait(barrier, peers + len(greeted))

    def copy_of(number, dy, dx):
        offset, count = plan.segments[(dy, dx)]
        return pltpu.make_async_remote_copy(
            src_ref=edge_ref.at[pl.ds(offset - plan.own_rows, count)],
            dst_ref=wide.at[pl.ds(offset, count)],
            send_sem=send_sem.at[number],
            recv_sem=recv_sem.at[number],
            device_id=place(-dy, -dx),
            device_id_type=MESH,
        )

    for number, (dy, dx) in enumerate(AROUND):
        when_there(-dy, lambda n=number, y=dy, x=dx: copy_of(n, y, x).start())
        if dy:
            offset, count = plan.segments[(dy, dx)]

            def clear(offset=offset, count=count):
                wide[pl.ds(offset, count), :] = jnp.zeros((count, wide.shape[1]), wide.dtype)

            pl.when(jnp.logical_not((lat > 0) if dy < 0 else (lat < lats - 1)))(clear)

    def finish():
        for number, (dy, dx) in enumerate(AROUND):
            when_there(dy, lambda n=number, y=dy, x=dx: copy_of(n, y, x).wait_recv())
            when_there(-dy, lambda n=number, y=dy, x=dx: copy_of(n, y, x).wait_send())

    return finish


def fill_bias(number_ref, parts_ref, bias):
    heads = bias.shape[0]
    entries = parts_ref.shape[1]
    parts = parts_ref[...]
    spots = lax.broadcasted_iota(jnp.int32, (entries, LANES), 0)
    for p in range(WIN):
        hot = jnp.where(spots == number_ref[p : p + 1, :], 1.0, 0.0).astype(jnp.bfloat16)
        terms = jnp.dot(parts, hot, preferred_element_type=jnp.float32)
        bias[:, p, :] = terms[:heads] + terms[heads : 2 * heads] + terms[2 * heads :]
    bias[:, WIN:, :] = jnp.zeros((heads, ROWS - WIN, LANES), jnp.float32)


def arrange_windows(plan, wide, gather_ref, gain_ref, normed, tags):
    features = normed.shape[1]
    everything = wide[...]
    for w in range(plan.windows):
        rows = pl.ds(w * ROWS, ROWS)
        chosen = pick(gather_ref[rows, :], everything)
        normed[rows, :] = normalize(chosen[:, :features], gain_ref[...])
        tags[rows, :] = chosen[:, features:]


def attend_windows(plan, inward_ref, bias_ref, normed, triple, tags, mixed, unroll, after=None):
    features = normed.shape[1]
    heads = bias_ref.shape[0]
    size = features // heads
    per_group = LANES // size
    groups = features // LANES

    step = 256
    for member in range(3):
        @pl.loop(0, features // step)
        def _(block):
            cols = pl.ds(pl.multiple_of(block * step, step), step)
            triple[member, :, cols] = jnp.dot(
                normed[...], inward_ref[member, :, cols], preferred_element_type=jnp.float32
            ).astype(jnp.bfloat16)

    owner = lax.broadcasted_iota(jnp.int32, (ROWS, LANES), 1) // size
    fill = jnp.zeros((LANES - ROWS, LANES), jnp.bfloat16)
    first = jnp.where(
        lax.broadcasted_iota(jnp.int32, (16, LANES), 1) == 0, 1.0, 0.0
    ).astype(jnp.bfloat16)

    def spread(block):
        parts = []
        for h in range(per_group):
            parts += [jnp.where(owner == h, block, jnp.zeros_like(block)), fill]
        return jnp.concatenate(parts, axis=0)

    head_of_row = lax.broadcasted_iota(jnp.int32, (per_group * LANES, LANES), 0) // LANES
    head_of_lane = lax.broadcasted_iota(jnp.int32, (per_group * LANES, LANES), 1) // size
    ones = jnp.where(head_of_row == head_of_lane, 1.0, 0.0).astype(jnp.bfloat16)

    @pl.loop(0, plan.windows)
    def _(w):
        rows = pl.ds(pl.multiple_of(w * ROWS, ROWS), ROWS)
        tag_block = tags[rows, :]
        across = lax.dot_general(
            first, jnp.concatenate([tag_block, fill], axis=0), NT, preferred_element_type=jnp.float32
        )
        allowed = tag_block[:, :1].astype(jnp.float32) == across[:1, :]

        @pl.loop(0, groups, unroll=unroll)
        def _(g):
            cols = pl.ds(pl.multiple_of(g * LANES, LANES), LANES)
            scores = lax.dot_general(
                triple[0, rows, cols], spread(triple[1, rows, cols]), NT, preferred_element_type=jnp.float32
            )
            weights = []
            for h in range(per_group):
                score = scores[:, h * LANES : (h + 1) * LANES] * size ** (-0.5)
                score = score + bias_ref[g * per_group + h]
                score = jnp.where(allowed, score, -1e30)
                weight = jnp.exp(score - jnp.max(score, axis=-1, keepdims=True))
                weights.append(weight.astype(jnp.bfloat16))
            weights = jnp.concatenate(weights, axis=1)
            blended = jnp.dot(weights, spread(triple[2, rows, cols]), preferred_element_type=jnp.float32)
            totals = jnp.dot(weights, ones, preferred_element_type=jnp.float32)
            mixed[rows, cols] = (blended / totals).astype(jnp.bfloat16)

        if after is not None:
            after(w)


def fine_kernel(
    plan, split, own_ref, edge_ref, tag_ref, gather_ref, scatter_ref, patch_ref, edge_index_ref, gain_ref,
    number_ref, parts_ref, coarse_parts_ref, merge_gain_ref, s0, s1, s2, s3, s4,
    fine_ref, coarse_ref, coarse_edge_ref, coarse_bias_ref, inward_two_ref, outward_two_ref,
    wide, normed, triple, tags, mixed, send_sem, recv_sem, bias_ref, inward_ref, outward_ref, merge_ref, *sems,
):
    features = normed.shape[1]
    shards = (s0, s1, s2, s3, s4)
    fulls = (inward_ref, outward_ref, merge_ref, inward_two_ref, outward_two_ref)
    gather = Gather(shards, fulls, split, sems)
    finish = exchange_halo(plan, edge_ref, wide, send_sem, recv_sem, gather.greeted())
    gather.begin()
    wide[: plan.own_rows, :] = own_ref[...]
    fill_bias(number_ref, parts_ref, bias_ref)
    finish()
    gather.step(0)
    arrange_windows(plan, wide, gather_ref, gain_ref, normed, tags)
    gather.step(1)
    gather.step(2)
    fill_bias(number_ref, coarse_parts_ref, coarse_bias_ref)
    gather.ready(0)
    last = gather.count + 2
    spots = {}
    for number in range(3, last):
        spots.setdefault(min((number - 3) * plan.windows // (last - 3) + 1, plan.windows - 1), []).append(number)

    def after(w):
        for spot, numbers in spots.items():
            @pl.when(w == spot)
            def _(numbers=numbers):
                for number in numbers:
                    gather.step(number)

    attend_windows(plan, inward_ref, bias_ref, normed, triple, tags, mixed, 2, after)
    gather.ready(1)
    own_mixed = pick(scatter_ref[...], mixed[...])
    update = lax.dot_general(own_mixed, outward_ref[0], NT, preferred_element_type=jnp.float32)
    fine = (own_ref[:, :features].astype(jnp.float32) + update).astype(jnp.bfloat16)
    fine_ref[...] = fine
    gather.ready(2)
    members = [pick(patch_ref[m], fine).astype(jnp.float32) for m in range(4)]
    count = 4 * features
    mean = sum(jnp.sum(m, axis=-1, keepdims=True) for m in members) / count
    centers = [m - mean for m in members]
    spread = sum(jnp.sum(c * c, axis=-1, keepdims=True) for c in centers) / count
    factor = lax.rsqrt(spread + EPSILON)
    merged = None
    for m in range(4):
        cols = slice(m * features, (m + 1) * features)
        part = (centers[m] * factor * merge_gain_ref[:, cols]).astype(jnp.bfloat16)
        term = lax.dot_general(part, merge_ref[0, :, cols], NT, preferred_element_type=jnp.float32)
        merged = term if merged is None else merged + term
    coarse = jnp.concatenate([merged.astype(jnp.bfloat16), tag_ref[...]], axis=1)
    coarse_ref[...] = coarse
    coarse_edge_ref[...] = pick(edge_index_ref[...], coarse)
    for number in range(3, gather.count):
        gather.ready(number)
    gather.end()


def coarse_kernel(
    plan, own_ref, edge_ref, gather_ref, scatter_ref, gain_ref, inward_ref, outward_ref, bias_ref,
    out_ref, wide, normed, triple, tags, mixed, send_sem, recv_sem,
):
    features = normed.shape[1]
    finish = exchange_halo(plan, edge_ref, wide, send_sem, recv_sem)
    wide[: plan.own_rows, :] = own_ref[...]
    finish()
    arrange_windows(plan, wide, gather_ref, gain_ref, normed, tags)
    attend_windows(plan, inward_ref, bias_ref, normed, triple, tags, mixed, 4)
    own_mixed = pick(scatter_ref[...], mixed[...])
    update = lax.dot_general(own_mixed, outward_ref[0], NT, preferred_element_type=jnp.float32)
    out_ref[...] = (own_ref[:, :features].astype(jnp.float32) + update).astype(jnp.bfloat16)


def level_scratch(plan, features):
    rows = plan.windows * ROWS
    return [
        pltpu.VMEM((plan.wide_rows, features + LANES), jnp.bfloat16),
        pltpu.VMEM((rows, features), jnp.bfloat16),
        pltpu.VMEM((3, rows, features), jnp.bfloat16),
        pltpu.VMEM((rows, LANES), jnp.bfloat16),
        pltpu.VMEM((rows, features), jnp.bfloat16),
        pltpu.SemaphoreType.DMA((len(AROUND),)),
        pltpu.SemaphoreType.DMA((len(AROUND),)),
    ]


class Gather:
    def __init__(self, shards, fulls, split, sems):
        self.shards, self.fulls, self.split, self.sems = shards, fulls, split, sems
        self.entries = weight_entries(shards)
        self.count = len(self.entries)
        self.index = {a: lax.axis_index(a) for a in ("grp", "lat", "lon", "lvl")}
        self.size = {a: lax.axis_size(a) for a in ("grp", "lat", "lon", "lvl")}
        self.halves = 2 if split else 1
        self.ways = [(d, half) for d in range(1, self.size["lon"]) for half in range(self.halves)]

    def at(self, axis, step):
        return {axis: lax.rem(self.index[axis] + step, self.size[axis])}

    def greeted(self):
        axes = ("lon", "lvl", "lat", "grp") if self.split else ("lon", "lvl")
        return [self.at(axis, d) for axis in axes for d in range(1, self.size[axis])]

    def place(self, n, lon_of, start, size):
        m, k, depth = self.entries[n]
        rows, cols = self.shards[m].shape[1:]
        return self.fulls[m].at[
            pl.ds(k, depth),
            pl.ds(pl.multiple_of(lon_of * rows + start, 16), size),
            pl.ds(pl.multiple_of(self.index["lvl"] * cols, cols), cols),
        ]

    def held(self, n, start, size):
        m, k, depth = self.entries[n]
        return self.shards[m].at[pl.ds(k, depth), pl.ds(start, size), :]

    def rows(self, n):
        return self.shards[self.entries[n][0]].shape[1]

    def source(self, d):
        return lax.rem(self.index["lon"] - d + self.size["lon"], self.size["lon"])

    def remote(self, src, dst, kind, number, device):
        send, recv = self.sems[1 + 2 * kind], self.sems[2 + 2 * kind]
        return pltpu.make_async_remote_copy(
            src_ref=src, dst_ref=dst, send_sem=send.at[number], recv_sem=recv.at[number],
            device_id=device, device_id_type=MESH,
        )

    def piece(self, n, half, grp_of, lat_of):
        rows = self.rows(n)
        if not self.split:
            return 0, rows
        grps, lats = self.size["grp"], self.size["lat"]
        size = rows // (2 * grps * lats)
        order = grp_of * lats + lat_of if half == 0 else lat_of * grps + grp_of
        start = half * (rows // 2) + order * size
        return pl.multiple_of(start, 16), size

    def mine(self, n, half):
        return self.piece(n, half, self.index["grp"], self.index["lat"])

    def axis_of(self, half, first):
        return "lat" if (half == 0) == first else "grp"

    def others(self, half, first):
        return range(1, self.size[self.axis_of(half, first)]) if self.split else ()

    def own_copy(self, n):
        return pltpu.make_async_copy(
            self.held(n, 0, self.rows(n)), self.place(n, self.index["lon"], 0, self.rows(n)), self.sems[0].at[n]
        )

    def lon_copy(self, n, d, half):
        start, size = self.mine(n, half)
        return self.remote(
            self.held(n, start, size), self.place(n, self.index["lon"], start, size),
            0, (n, d - 1, half), self.at("lon", d),
        )

    def one_copy(self, n, d, half, e):
        start, size = self.mine(n, half)
        block = self.place(n, self.source(d), start, size)
        return self.remote(block, block, 1, (n, d - 1, half, e - 1), self.at(self.axis_of(half, True), e))

    def two_copy(self, n, d, half, e):
        if half == 0:
            start, size = self.piece(n, half, self.index["grp"], 0)
            size *= self.size["lat"]
        else:
            start, size = self.piece(n, half, 0, self.index["lat"])
            size *= self.size["grp"]
        block = self.place(n, self.source(d), start, size)
        return self.remote(block, block, 2, (n, d - 1, half, e - 1), self.at(self.axis_of(half, False), e))

    def lvl_copy(self, n, d, e):
        block = self.place(n, self.source(d), 0, self.rows(n))
        src = block if d else self.held(n, 0, self.rows(n))
        return self.remote(src, block, 3, (n, d, e - 1), self.at("lvl", e))

    def siblings(self):
        return range(1, self.size["lvl"])

    def begin(self):
        for n in range(self.count):
            self.own_copy(n).start()
            for d, half in self.ways:
                self.lon_copy(n, d, half).start()
            for e in self.siblings():
                self.lvl_copy(n, 0, e).start()

    def step(self, s):
        if s < self.count:
            for d, half in self.ways:
                self.lon_copy(s, d, half).wait_recv()
                for e in self.others(half, True):
                    self.one_copy(s, d, half, e).start()
        if 0 <= s - 1 < self.count:
            for d, half in self.ways:
                for e in self.others(half, True):
                    self.one_copy(s - 1, d, half, e).wait_recv()
                for e in self.others(half, False):
                    self.two_copy(s - 1, d, half, e).start()
        if 0 <= s - 2 < self.count:
            for d in range(1, self.size["lon"]):
                for half in range(self.halves):
                    for e in self.others(half, False):
                        self.two_copy(s - 2, d, half, e).wait_recv()
                for e in self.siblings():
                    self.lvl_copy(s - 2, d, e).start()

    def ready(self, n):
        self.own_copy(n).wait()
        for d in range(self.size["lon"]):
            for e in self.siblings():
                self.lvl_copy(n, d, e).wait_recv()

    def end(self):
        for n in range(self.count):
            for d in range(self.size["lon"]):
                for e in self.siblings():
                    self.lvl_copy(n, d, e).wait_send()
            for d, half in self.ways:
                self.lon_copy(n, d, half).wait_send()
                for e in self.others(half, True):
                    self.one_copy(n, d, half, e).wait_send()
                for e in self.others(half, False):
                    self.two_copy(n, d, half, e).wait_send()


def weight_entries(weights):
    result = []
    for m, w in enumerate(weights):
        each = w.shape[0] if m == 0 else 1
        result += [(m, k, each) for k in range(0, w.shape[0], each)]
    return result


def gather_scratch(weights, split):
    grps, lats, lons, lvls = (lax.axis_size(a) for a in ("grp", "lat", "lon", "lvl"))
    count = len(weight_entries(weights))
    halves = 2 if split else 1
    most = max(grps, lats) - 1 if split else 1
    dma = pltpu.SemaphoreType.DMA
    return (
        [dma((count,))]
        + [dma((count, lons - 1, halves))] * 2
        + [dma((count, lons - 1, halves, most))] * 4
        + [dma((count, lons, lvls - 1))] * 2
    )


def offset_numbers():
    p = np.arange(WIN)
    r, c = p // WIN_LON, p % WIN_LON
    number = (r[:, None] - r[None, :] + WIN_LAT - 1) * (2 * WIN_LON - 1) + c[:, None] - c[None, :] + WIN_LON - 1
    result = np.full((ROWS, LANES), -1, np.int32)
    result[:WIN, :WIN] = number
    return result


def table_parts(table):
    terms, rest = [], table
    for _ in range(3):
        term = lax.reduce_precision(rest, 8, 7)
        terms.append(term.astype(jnp.bfloat16))
        rest = rest - term
    parts = jnp.concatenate(terms, axis=0)
    return jnp.pad(parts, ((0, 0), (0, up_to(parts.shape[1], LANES) - parts.shape[1])))


def shards(
    tokens, fine_tags, coarse_tags, fine_gain, fine_inward, fine_outward, fine_table, merge_gain,
    merge_weight, coarse_gain, coarse_inward, coarse_outward, coarse_table,
):
    _, lat_len, lon_len, width = tokens.shape
    fine_plan, coarse_plan = Plan(lat_len, lon_len), Plan(lat_len // 2, lon_len // 2)
    weights = [fine_inward, fine_outward[None], merge_weight[None], coarse_inward, coarse_outward[None]]
    grps, lats, lons, lvls = (lax.axis_size(a) for a in ("grp", "lat", "lon", "lvl"))
    split = all(w.shape[1] % (2 * grps * lats * 16) == 0 for w in weights)
    wholes = [(w.shape[0], w.shape[1] * lons, w.shape[2] * lvls) for w in weights]

    tagged = jnp.concatenate(
        [tokens[0], jnp.broadcast_to(fine_tags[0, :, :, None], (lat_len, lon_len, LANES)).astype(jnp.bfloat16)], axis=2
    )
    own = tagged.reshape(lat_len * lon_len, -1)
    own = jnp.pad(own, ((0, fine_plan.own_rows - fine_plan.own), (0, 0)))
    pieces = []
    for dy, dx in AROUND:
        part = tagged
        part = part[-HALF_LAT:] if dy < 0 else (part[:HALF_LAT] if dy > 0 else part)
        part = part[:, -HALF_LON:] if dx < 0 else (part[:, :HALF_LON] if dx > 0 else part)
        part = part.reshape(-1, part.shape[2])
        pieces.append(jnp.pad(part, ((0, up_to(part.shape[0], 16) - part.shape[0]), (0, 0))))
    edge = jnp.concatenate(pieces, axis=0)
    coarse_width = wholes[2][1]
    coarse_marks = jnp.broadcast_to(coarse_tags.reshape(-1, 1), (coarse_plan.own, LANES)).astype(jnp.bfloat16)
    coarse_marks = jnp.pad(coarse_marks, ((0, coarse_plan.own_rows - coarse_plan.own), (0, 0)))

    edge_rows = coarse_plan.wide_rows - coarse_plan.own_rows
    heads, coarse_heads = fine_table.shape[0], coarse_table.shape[0]
    fine, coarse_own, coarse_edge, coarse_bias, inward_two, outward_two = pl.pallas_call(
        functools.partial(fine_kernel, fine_plan, split),
        out_shape=[
            jax.ShapeDtypeStruct((fine_plan.own_rows, width), jnp.bfloat16),
            jax.ShapeDtypeStruct((coarse_plan.own_rows, coarse_width + LANES), jnp.bfloat16),
            jax.ShapeDtypeStruct((edge_rows, coarse_width + LANES), jnp.bfloat16),
            jax.ShapeDtypeStruct((coarse_heads, ROWS, LANES), jnp.float32),
            jax.ShapeDtypeStruct(wholes[3], jnp.bfloat16),
            jax.ShapeDtypeStruct(wholes[4], jnp.bfloat16),
        ],
        in_specs=[VMEM] * 12 + [ANY] * 5,
        out_specs=[VMEM] * 6,
        scratch_shapes=level_scratch(fine_plan, width)
        + [pltpu.VMEM((heads, ROWS, LANES), jnp.float32)]
        + [pltpu.VMEM(shape, jnp.bfloat16) for shape in wholes[:3]]
        + gather_scratch(weights, split),
        compiler_params=pltpu.CompilerParams(collective_id=1, has_side_effects=True, vmem_limit_bytes=LIMIT),
        name="fine_level",
    )(
        own, edge, coarse_marks, fine_plan.gather, fine_plan.scatter, fine_plan.patches(),
        coarse_plan.edges(), fine_gain[None], offset_numbers(), table_parts(fine_table),
        table_parts(coarse_table), merge_gain[None], *weights,
    )
    coarse = pl.pallas_call(
        functools.partial(coarse_kernel, coarse_plan),
        out_shape=jax.ShapeDtypeStruct((coarse_plan.own_rows, coarse_width), jnp.bfloat16),
        in_specs=[VMEM] * 8,
        out_specs=VMEM,
        scratch_shapes=level_scratch(coarse_plan, coarse_width),
        compiler_params=pltpu.CompilerParams(collective_id=2, has_side_effects=True, vmem_limit_bytes=LIMIT),
        name="coarse_level",
    )(
        coarse_own, coarse_edge, coarse_plan.gather, coarse_plan.scatter, coarse_gain[None],
        inward_two, outward_two, coarse_bias,
    )
    fine = fine[: fine_plan.own].reshape(tokens.shape)
    coarse = coarse[: coarse_plan.own].reshape(1, lat_len // 2, lon_len // 2, coarse_width)
    return fine, coarse


def solution(mesh):
    placed = (
        P(("grp", "lvl"), "lat", "lon", None),
        P(("grp", "lvl"), "lat", "lon"),
        P(("grp", "lvl"), "lat", "lon"),
        P(),
        P(None, "lon", "lvl"),
        P("lon", "lvl"),
        P(),
        P(),
        P("lon", "lvl"),
        P(),
        P(None, "lon", "lvl"),
        P("lon", "lvl"),
        P(),
    )
    return jax.shard_map(
        shards,
        mesh=mesh,
        in_specs=placed,
        out_specs=(P(("grp", "lvl"), "lat", "lon", None), P(("grp", "lvl"), "lat", "lon", None)),
        check_vma=False,
    )
```

time: 210 us -> 142 us (0.68)
  local copies, waits for them, and re-layouts: 42 us -> 4.51 us
  Pallas kernels: 162 us -> 128 us
  other arithmetic: 4.24 us -> 8.45 us
    pallas_call x2 -> x1, Pallas kernels: 123 us -> 89.7 us  [shards(): pl.pallas_call(functools.partial(fine_kernel, fine_plan, split), out_shap...]
    another operation x2 -> x0, local copies, waits for them, and re-layouts: 12.5 us -> none  [bias_blocks(): jnp.stack([lax.slice_in_dim(grid, k, k + WIN_LON, axis=2)[:, :, ::-1] for...]
    concatenate x14 -> x0, local copies, waits for them, and re-layouts: 10.5 us -> none  [the longest x12 7.34 us: bias_blocks(): rows.append(jnp.concatenate(parts, axis=2))]
    rev x24 -> x0, local copies, waits for them, and re-layouts: 9.05 us -> none  [bias_blocks(): lax.slice_in_dim(grid, k, k + WIN_LON, axis=2)[:, :, ::-1]]
where the time goes in v2:
time: 142 us; the launch traced here: 141 us
  Pallas kernels  128 us (90%)
  other arithmetic  8.45 us (6%)
  local copies, waits for them, and re-layouts  4.51 us (3%)
    pallas_call x1, Pallas kernels, shards(): pl.pallas_call(functools.partial(fine_kernel, fine_plan, split), out_shap...  89.7 us
    pallas_call x1, Pallas kernels, shards(): pl.pallas_call(functools.partial(coarse_kernel, coarse_plan), out_shape=j...  37.9 us
    concatenate x4, other arithmetic, shards(): jnp.concatenate([tokens[0], jnp.broadcast_to(fine_tags[0, :, :, None], (l...  3.53 us

profile of v2, /device:TPU:0, one launch (start us, length us, event | category | flops | bytes accessed | tf_op | source)
XLA Modules:
  0.0 141.3 jit_solution(11918412111537769108)
XLA Ops:
  0.6 0.0 copy-start
  0.6 0.7 convert_reduce_fusion
  1.4 0.1 convert_element_type.56
  1.5 0.7 convert_reduce_fusion.1
  2.2 0.1 convert_element_type.53
  2.3 0.7 convert_element_type.52
  3.0 0.7 pad.49.tag_ref
  3.7 0.7 reduce-precision_convert_fusion.3
  4.4 0.6 fusion.18.parts_ref
  5.0 0.8 reduce-precision_convert_fusion.1
  5.8 0.6 fusion.8.coarse_parts_ref
  6.5 0.1 broadcast_in_dim.29
  6.6 0.1 broadcast_in_dim.28
  6.7 0.8 pad_maximum_fusion.1
  7.6 0.9 fusion.6
  8.5 1.0 fusion.1
  9.6 0.0 copy-done
  9.6 0.8 pad_maximum_fusion.own_ref
  10.5 0.0 copy-start.1
  10.6 0.8 copy-done.1
  11.4 89.7 %fine_level.1 = (bf16[288,512]{1,0:T(8,128)(2,1)}, bf16[80,1152]{1,0:T(8,128)(2,1)}, bf16[320,1152]{1,0:T(8,128)(2,1)}, f32[32,80,128]{2,1,0:T(8,128)}, bf16[3,1...) custom-call(bf16[288,640]{1,0:T(8,128)(2,1)} %pad_maximum_fusion.own_ref, bf16[448,640]{1,0:T(8,128)(2,1)} %copy-done.1, ...), custom_call_target="tpu_custom_call" | custom-call | tf_op jit(solution)/shard_map/fine_level/pallas_call | solution.py:553
  101.1 0.0 copy-start.2
  101.1 37.9 %coarse_level.1 = bf16[80,1024]{1,0:T(8,128)(2,1)} custom-call(bf16[80,1152]{1,0:T(8,128)(2,1)} %get-tuple-element.9.own_ref, bf16[320,1152]{1,0:T(8,128)(2,1)} %get-tuple-element.10.edge_ref, s32[320,1]{1,0:T(8,128)} %constant.22.clone.gather_ref, s32[80,1]{1,0:T(8,128)} %constant.23.clone.scatter_ref, f32[1,1024]{1,0:T(1,128)} %bitcast.26, ...), custom_call_target="tpu_custom_call" | custom-call | tf_op jit(solution)/shard_map/coarse_level/pallas_call | solution.py:576
  139.0 0.9 slice.43
  139.9 0.7 reshape.55
  140.6 0.0 copy-done.2
  140.6 0.7 copy.33
  (16 shorter events, 0.3 us)
Async XLA Ops:
  0.6 9.0 %copy-start = (bf16[1,12,24,512]{3,2,1,0:T(8,128)(2,1)S(1)}, bf16[1,12,24,512]{3,2,1,0:T(8,128)(2,1)}, u32[]{:S(2)}) copy-start(bf16[1,12,24,512]{3,2,1,0:T(8,128)(2,1)} %param.20) | copy-start | bytes 884740
  10.5 0.8 copy-start.1
  101.1 39.5 %copy-start.2 = (bf16[288,512]{1,0:T(8,128)(2,1)S(1)}, bf16[288,512]{1,0:T(8,128)(2,1)}, u32[]{:S(2)}) copy-start(bf16[288,512]{1,0:T(8,128)(2,1)} %get-tuple-element.8) | copy-start | bytes 884740
